TPU v7x, 32 devices: a whole 2x2x4 slice. The times are simulated.
32 devices in a mesh: dp: 2 (over x), row: 4 (over z), col: 4 (over y, core).
Axes of the slice: x: 2, y: 2, z: 4, core: 2. Of those that a mesh axis runs over, the one named last changes fastest.
Arguments:
- x: bfloat16 [256, 4096], P('dp', ('row', 'col')), parts along dimension 0
- ln_gain: bfloat16 [4096], P(('row', 'col'))
- w_in: bfloat16 [4096, 37376], P('row', 'col')
- w_out: bfloat16 [20480, 4096], P('col', 'row')
- k_cache: bfloat16 [256, 2048, 256], P(('dp', 'col', 'row')), parts along dimension 0
- v_cache: bfloat16 [256, 2048, 256], P(('dp', 'col', 'row')), parts along dimension 0
- lengths: int32 [256], P(('dp', 'col', 'row')), parts along dimension 0
- rope_cos: float32 [256, 128], P(('dp', 'col', 'row')), parts along dimension 0
- rope_sin: float32 [256, 128], P(('dp', 'col', 'row')), parts along dimension 0
Outputs:
- output 1: bfloat16 [256, 4096], P('dp', ('row', 'col')), parts along dimension 0
- output 2: bfloat16 [256, 2048, 256], P(('dp', 'col', 'row')), parts along dimension 0
- output 3: bfloat16 [256, 2048, 256], P(('dp', 'col', 'row')), parts along dimension 0
There are 2 independent parts. A program takes and returns all parts, laid end to end along the dimension named above; an argument that names none is the same for every part.
All inputs are finite; a program needn't handle non-finite values.
Results may differ from a plain program's by a relative error of at most 0.00926775.
Values are sent between devices in bfloat16 or wider.
A program may use at most 1 GiB of HBM per device.

v0:
```python
import jax
import jax.numpy as jnp
from jax import lax
from jax.sharding import PartitionSpec as P

NORM_EPS = 1e-6


def apply_rope(vals, cos_t, sin_t):
    half = vals.shape[-1] // 2
    first = vals[..., :half]
    second = vals[..., half:]
    return jnp.concatenate([first * cos_t - second * sin_t, second * cos_t + first * sin_t], axis=-1)


def local_attention(joined, k_cache, v_cache, lengths, rope_cos, rope_sin, q_cols, kv_cols):
    seq_count = joined.shape[0]
    col_count = joined.shape[1]
    head = rope_cos.shape[1] * 2
    heads = q_cols * col_count // head
    cache_len = k_cache.shape[1]
    q_raw = joined[:, :, :q_cols].reshape(seq_count, heads, head).astype(jnp.float32)
    k_raw = joined[:, :, q_cols:q_cols + kv_cols].reshape(seq_count, head).astype(jnp.float32)
    v_new = joined[:, :, q_cols + kv_cols:].reshape(seq_count, head)
    queries = (apply_rope(q_raw, rope_cos[:, None, :], rope_sin[:, None, :]) * head ** -0.5).astype(jnp.bfloat16)
    k_new = apply_rope(k_raw, rope_cos, rope_sin).astype(jnp.bfloat16)
    positions = jnp.arange(cache_len)
    new_slot = (positions[None, :] == lengths[:, None])[:, :, None]
    k_out = jnp.where(new_slot, k_new[:, None, :], k_cache)
    v_out = jnp.where(new_slot, v_new[:, None, :], v_cache)
    scores = jnp.einsum('bhd,btd->bht', queries, k_out, preferred_element_type=jnp.float32)
    visible = positions[None, None, :] <= lengths[:, None, None]
    attn_probs = jax.nn.softmax(jnp.where(visible, scores, -1e30), axis=-1).astype(jnp.bfloat16)
    attn_out = jnp.einsum('bht,btd->bhd', attn_probs, v_out, preferred_element_type=jnp.float32).astype(jnp.bfloat16)
    return attn_out.reshape(seq_count, col_count, q_cols).transpose(1, 0, 2), k_out, v_out


def solution(mesh):
    rows = mesh.shape['row']
    cols = mesh.shape['col']
    seq_spec = P(('dp', 'col', 'row'))
    act_spec = P('dp', ('row', 'col'))

    def local_layer(x, ln_gain, w_in, w_out, k_cache, v_cache, lengths, rope_cos, rope_sin):
        batch = x.shape[0]
        seq_count = batch // (rows * cols)
        width = x.shape[1] * rows * cols
        head = rope_cos.shape[1] * 2
        e_cols = w_in.shape[1]
        r_cols = w_out.shape[0]
        kv_cols = head // cols
        f_cols = e_cols - r_cols - 2 * kv_cols
        q_cols = r_cols - f_cols
        gate_start = q_cols + 2 * kv_cols
        x_float = x.astype(jnp.float32)
        row_stats = jnp.stack([x_float.sum(axis=1), jnp.square(x_float).sum(axis=1)], axis=1)
        row_stats = lax.psum(row_stats, ('row', 'col'))
        mean = row_stats[:, 0:1] / width
        variance = row_stats[:, 1:2] / width - jnp.square(mean)
        normed = ((x_float - mean) * lax.rsqrt(variance + NORM_EPS) * ln_gain.astype(jnp.float32)).astype(jnp.bfloat16)
        h_row = lax.all_gather(normed, 'col', axis=1, tiled=True)
        part_in = jnp.dot(h_row, w_in, preferred_element_type=jnp.float32).astype(jnp.bfloat16)
        projected = lax.psum(part_in, 'row')
        head_in = projected[:, :gate_start].reshape(cols, rows, seq_count, gate_start)
        head_in = lax.dynamic_index_in_dim(head_in, lax.axis_index('row'), axis=1, keepdims=False)
        joined = lax.all_to_all(head_in, 'col', 0, 0, tiled=True).transpose(1, 0, 2)
        attn_parts, k_out, v_out = local_attention(joined, k_cache, v_cache, lengths, rope_cos, rope_sin, q_cols, kv_cols)
        attn_parts = lax.all_to_all(attn_parts, 'col', 0, 0, tiled=True)
        attn_rows = lax.all_gather(attn_parts, 'row', axis=1).reshape(batch, q_cols)
        gate_in = projected[:, gate_start:gate_start + f_cols].astype(jnp.float32)
        up_in = projected[:, gate_start + f_cols:].astype(jnp.float32)
        mixed = (jax.nn.silu(gate_in) * up_in).astype(jnp.bfloat16)
        out_inputs = jnp.concatenate([attn_rows, mixed], axis=1)
        part_out = jnp.dot(out_inputs, w_out, preferred_element_type=jnp.float32).astype(jnp.bfloat16)
        delta = lax.psum_scatter(part_out, 'col', scatter_dimension=1, tiled=True)
        y = (x_float + delta.astype(jnp.float32)).astype(jnp.bfloat16)
        return y, k_out, v_out

    return jax.shard_map(local_layer, mesh=mesh, in_specs=(act_spec, P(('row', 'col')), P('row', 'col'), P('col', 'row'), seq_spec, seq_spec, seq_spec, seq_spec, seq_spec), out_specs=(act_spec, seq_spec, seq_spec), check_vma=False)
```

profile of v0, /device:TPU:0, one launch (start us, length us, event | category | flops | bytes accessed | tf_op | source)
XLA Modules:
  0.0 238.6 jit_solution(2288549023745095923)
XLA Ops:
  7.2 0.7 convert_element_type.57
  7.9 1.0 convert_reduce_fusion
  8.8 35.0 %psum.14 = f32[128,2]{0,1:T(2,128)S(1)} all-reduce(f32[128,2]{0,1:T(2,128)S(1)} %pad_maximum_fusion.1), channel_id=1, replica_groups=mesh['dp'=2,'row'=4,'col'=4] {'row','col'}, use_global_device_ids=true, to_apply=%region_2.0 | all-reduce | flops 256 | bytes 2048 | tf_op jit(solution)/shard_map/psum | solution.py:57
  43.8 0.9 fusion.19
  44.8 5.8 %all_gather.9 = bf16[128,1024]{1,0:T(8,128)(2,1)S(1)} all-gather(bf16[128,256]{1,0:T(8,128)(2,1)S(1)} %fusion.19), channel_id=1, replica_groups=mesh['dp'=2,'row'=4,'col'=4] {'col'}, dimensions={1}, use_global_device_ids=true | all-gather | bytes 327680 | tf_op jit(solution)/shard_map/all_gather | solution.py:61
  50.6 10.6 %convolution_convert_fusion = bf16[128,9344]{1,0:T(8,128)(2,1)} fusion(bf16[128,1024]{1,0:T(8,128)(2,1)S(1)} %all_gather.9, bf16[1024,9344]{1,0:T(8,128)(2,1)} %param.11), kind=kOutput, calls=%fused_computation.1 | convolution fusion | flops 2450669568 | bytes 21790720 | tf_op jit(solution)/shard_map/dot_general | solution.py:62
  61.2 92.7 %all-reduce.2.cloned.1.call-done = bf16[128,9344]{1,0:T(8,128)(2,1)} async-done(((bf16[128,9344]{1,0:T(8,128)(2,1)}), bf16[128,9344]{1,0:T(8,128)(2,1)}) %all-reduce.2.cloned.1.call-update) | async-done | bytes 2392080 | tf_op jit(solution)/shard_map/psum | solution.py:63
  153.9 1.0 slice.48
  154.9 0.6 dynamic-slice_bitcast_fusion
  155.5 3.3 %all-to-all-start = ((bf16[4,8,1152]{2,1,0:T(8,128)(2,1)}), bf16[4,8,1152]{2,1,0:T(8,128)(2,1)S(1)}, u32[]{:S(2)}, u32[]{:S(2)}) async-start(bf16[4,8,1152]{2,1,0:T(8,128)(2,1)} %dynamic-slice_bitcast_fusion), calls=%async_computation | async-start | bytes 147456 | tf_op jit(solution)/shard_map/all_to_all | solution.py:66
  158.9 3.8 %all-to-all-done = bf16[4,8,1152]{2,1,0:T(8,128)(2,1)S(1)} async-done(((bf16[4,8,1152]{2,1,0:T(8,128)(2,1)}), bf16[4,8,1152]{2,1,0:T(8,128)(2,1)S(1)}, u32[]{:S(2)}, u32[]{:S(2)}) %all-to-all-start) | async-done | bytes 73760 | tf_op jit(solution)/shard_map/all_to_all | solution.py:66
  163.3 9.8 %broadcast_select_fusion.1 = (bf16[8,2048,256]{2,1,0:T(8,128)(2,1)S(1)}, bf16[8,2048,256]{2,1,0:T(8,128)(2,1)}) fusion(bf16[8,2048,256]{2,1,0:T(8,128)(2,1)} %param.13, pred[8,2048]{1,0:T(8,128)(4,1)S(1)} %get-tuple-element.16, bf16[8,256]{1,0:T(8,128)(2,1)S(1)} %pad_maximum_fusion, bf16[8,2048,256]{2,1,0:T(8,128)(2,1)} %param.14, ...), kind=kLoop, calls=%fused_computation.3 | loop fusion | flops 8388608 | bytes 33579008 | tf_op jit(solution)/shard_map/jit(_where)/select_n | solution.py:29
  173.0 3.4 %copy-done = bf16[8,2048,256]{2,1,0:T(8,128)(2,1)} copy-done((bf16[8,2048,256]{2,1,0:T(8,128)(2,1)}, bf16[8,2048,256]{2,1,0:T(8,128)(2,1)S(1)}, u32[]{:S(2)}) %copy-start) | copy-done | bytes 8388632
  176.4 2.3 convolution_select_fusion
  178.7 0.3 fusion.29
  179.0 4.7 %convolution_convert_fusion.1 = bf16[8,16,256]{2,1,0:T(8,128)(2,1)S(1)} fusion(bf16[8,2048,256]{2,1,0:T(8,128)(2,1)} %get-tuple-element.10, f32[8,16]{1,0:T(8,128)S(1)} %fusion.29, f32[8,16,2048]{2,1,0:T(8,128)S(1)} %convolution_select_fusion), kind=kOutput, calls=%fused_computation.19 | convolution fusion | flops 135039104 | bytes 9503232 | tf_op jit(solution)/shard_map/bht,btd->bhd/dot_general | solution.py:34
  183.8 0.7 copy.23
  184.4 3.3 %all-to-all-start.1 = ((bf16[4,8,1024]{2,1,0:T(8,128)(2,1)}), bf16[4,8,1024]{2,1,0:T(8,128)(2,1)S(1)}, u32[]{:S(2)}, u32[]{:S(2)}) async-start(bf16[4,8,1024]{2,1,0:T(8,128)(2,1)} %bitcast.22), calls=%async_computation.1 | async-start | bytes 131072 | tf_op jit(solution)/shard_map/all_to_all | solution.py:68
  187.8 0.6 fusion.7
  188.4 3.2 %all-to-all-done.1 = bf16[4,8,1024]{2,1,0:T(8,128)(2,1)S(1)} async-done(((bf16[4,8,1024]{2,1,0:T(8,128)(2,1)}), bf16[4,8,1024]{2,1,0:T(8,128)(2,1)S(1)}, u32[]{:S(2)}, u32[]{:S(2)}) %all-to-all-start.1) | async-done | bytes 65568 | tf_op jit(solution)/shard_map/all_to_all | solution.py:68
  191.6 13.9 %all-gather = bf16[4,32,1024]{2,1,0:T(8,128)(2,1)S(1)} all-gather(bf16[4,8,1024]{2,1,0:T(8,128)(2,1)S(1)} %all-to-all-done.1), channel_id=2, replica_groups=mesh['dp'=2,'row'=4,'col'=4] {'row'}, dimensions={1}, use_global_device_ids=true | all-gather | bytes 327680 | tf_op jit(solution)/shard_map/all_gather | solution.py:69
  205.5 6.2 %fusion.12 = bf16[128,1024]{1,0:T(8,128)(2,1)} fusion(bf16[5120,1024]{1,0:T(8,128)(2,1)} %param.12, bf16[128,4096]{1,0:T(8,128)(2,1)S(1)} %fusion.7, bf16[128,1024]{1,0:T(8,128)(2,1)S(1)} %bitcast.26), kind=kOutput, calls=%fused_computation.18 | convolution fusion | flops 1344929792 | bytes 12058624 | tf_op jit(solution)/shard_map/dot_general | solution.py:74
  211.7 18.6 %reduce-scatter.2.cloned.1.call-done = bf16[128,256]{1,0:T(8,128)(2,1)} async-done(((bf16[128,1024]{1,0:T(8,128)(2,1)}), bf16[128,256]{1,0:T(8,128)(2,1)}) %reduce-scatter.2.cloned.1.call-update) | async-done | bytes 65552 | tf_op jit(solution)/shard_map/reduce_scatter | solution.py:75
  230.3 1.5 fusion.20
  (30 shorter events, 0.7 us)
Async XLA Ops:
  7.2 146.7 %all-reduce.2.cloned.1.call-start = ((), (), s32[]{:S(2)}) async-start(), calls=%async_computation.3 | async-start | bytes 4784128 | tf_op jit(solution)/shard_map/psum | solution.py:63
  50.6 108.3 %copy-start.5 = (s32[8]{0:T(128)S(1)}, s32[8]{0:T(128)}, u32[]{:S(2)}) copy-start(s32[8]{0:T(128)} %param.15) | copy-start | bytes 100
  50.6 112.6 %copy-start.3 = (f32[8,128]{1,0:T(8,128)S(1)}, f32[8,128]{1,0:T(8,128)}, u32[]{:S(2)}) copy-start(f32[8,128]{1,0:T(8,128)} %param.17) | copy-start | bytes 12292
  50.6 112.6 %copy-start.4 = (f32[8,128]{1,0:T(8,128)S(1)}, f32[8,128]{1,0:T(8,128)}, u32[]{:S(2)}) copy-start(f32[8,128]{1,0:T(8,128)} %param.16) | copy-start | bytes 12292
  155.5 7.2 %all-to-all-start = ((bf16[4,8,1152]{2,1,0:T(8,128)(2,1)}), bf16[4,8,1152]{2,1,0:T(8,128)(2,1)S(1)}, u32[]{:S(2)}, u32[]{:S(2)}) async-start(bf16[4,8,1152]{2,1,0:T(8,128)(2,1)} %dynamic-slice_bitcast_fusion), calls=%async_computation | async-start | bytes 147456 | tf_op jit(solution)/shard_map/all_to_all | solution.py:66
  173.0 3.4 %copy-start = (bf16[8,2048,256]{2,1,0:T(8,128)(2,1)}, bf16[8,2048,256]{2,1,0:T(8,128)(2,1)S(1)}, u32[]{:S(2)}) copy-start(bf16[8,2048,256]{2,1,0:T(8,128)(2,1)S(1)} %get-tuple-element.9) | copy-start | bytes 25165828
  176.4 11.3 %copy-start.1 = (bf16[128,9344]{1,0:T(8,128)(2,1)S(1)}, bf16[128,9344]{1,0:T(8,128)(2,1)}, u32[]{:S(2)}) copy-start(bf16[128,9344]{1,0:T(8,128)(2,1)} %all-reduce.2.cloned.1.call-done) | copy-start | bytes 7176196
  184.4 7.2 %all-to-all-start.1 = ((bf16[4,8,1024]{2,1,0:T(8,128)(2,1)}), bf16[4,8,1024]{2,1,0:T(8,128)(2,1)S(1)}, u32[]{:S(2)}, u32[]{:S(2)}) async-start(bf16[4,8,1024]{2,1,0:T(8,128)(2,1)} %bitcast.22), calls=%async_computation.1 | async-start | bytes 131072 | tf_op jit(solution)/shard_map/all_to_all | solution.py:68
  187.7 42.6 %reduce-scatter.2.cloned.1.call-start = ((), (), s32[]{:S(2)}) async-start(), calls=%async_computation.4 | async-start | bytes 327680 | tf_op jit(solution)/shard_map/reduce_scatter | solution.py:75
  205.5 24.8 %copy-start.2 = (bf16[128,256]{1,0:T(8,128)(2,1)S(1)}, bf16[128,256]{1,0:T(8,128)(2,1)}, u32[]{:S(2)}) copy-start(bf16[128,256]{1,0:T(8,128)(2,1)} %param.9) | copy-start | bytes 196612
Sparse Core Ops, SparseCore 0:
  61.3 92.5 all-reduce.1
  211.8 18.3 reduce-scatter.1
where the time goes:
time: 239 us
  waiting for transfers between devices  118 us (49%)
  blocking collectives  54.6 us (23%)
  matrix products  23.8 us (10%)
  other arithmetic  15 us (6%)
  between operations  14.2 us (6%)
  starting transfers between devices  6.65 us (3%)
  local copies, waits for them, and re-layouts  6.08 us (3%)
    psum x1, waiting for transfers between devices, local_layer(): projected = lax.psum(part_in, 'row')  92.7 us
    psum x1, blocking collectives, local_layer(): row_stats = lax.psum(row_stats, ('row', 'col'))  35 us
    reduce_scatter x1, waiting for transfers between devices, local_layer(): delta = lax.psum_scatter(part_out, 'col', scatter_dimension=1, tiled=True)  18.6 us
    all_gather x1, blocking collectives, local_layer(): attn_rows = lax.all_gather(attn_parts, 'row', axis=1).reshape(batch, q_cols)  13.9 us
    dot_general x1, matrix products, local_layer(): jnp.dot(h_row, w_in, preferred_element_type=jnp.float32)  10.6 us
    select_n x1, other arithmetic, local_attention(): k_out = jnp.where(new_slot, k_new[:, None, :], k_cache)  9.76 us
    dot_general x1, matrix products, local_layer(): jnp.dot(out_inputs, w_out, preferred_element_type=jnp.float32)  6.23 us
    all_gather x1, blocking collectives, local_layer(): h_row = lax.all_gather(normed, 'col', axis=1, tiled=True)  5.78 us
  transfers between devices with their start and end apart: 4, of which 4 were waited for; matrix products, arithmetic and copies ran while one was open for 0% of the time, Pallas kernels for 0%

commit v1 on v0

v1 whole, which is shorter than its diff:
```python
import functools

import jax
import jax.numpy as jnp
from jax import lax
from jax.experimental import pallas as pl
from jax.experimental.pallas import tpu as pltpu
from jax.sharding import PartitionSpec as P

NORM_EPS = 1e-6
MESH = pl.DeviceIdType.MESH
F32 = jnp.float32
BF16 = jnp.bfloat16
CHUNK = 128
LEAD = 3
GAIN_ROWS = 16


def layer_kernel(dims, xs_ref, win_ref, wout_ref, kc_ref, vc_ref, len_ref, cos_ref, sin_ref,
                 y_ref, knew_ref, vnew_ref,
                 wq, wgu, wo, kbuf, vbuf, xg, st, h, part, rbuf, mful, qsend, qrecv, qhm, qsm, kn3, vn3, osm,
                 asend, arecv, acc, ysend, yrecv,
                 wsem, kvsem, xs_s, xs_r, st_s, st_r, q_s, q_r, rs_s, rs_r, ag_s, ag_r, at_s, at_r, y_s, y_r):
    rows, cols, n_chunks, w, q_cols, kv_cols, f_cols = dims
    group = rows * cols
    dp, r, c = lax.axis_index("dp"), lax.axis_index("row"), lax.axis_index("col")
    me = c * rows + r
    batch, xw = y_ref.shape
    seqs = batch // group
    gate_start = q_cols + 2 * kv_cols
    half_f = f_cols // 2
    heads_c = q_cols // 256
    heads = heads_c * cols
    cache_len = kbuf.shape[1]

    def dev(g):
        return (dp, g % rows, g // rows)

    def wq_copy():
        return pltpu.make_async_copy(win_ref.at[:, pl.ds(0, gate_start)], wq, wsem.at[4 * n_chunks])

    def wgu_copy(d, k, part_id):
        col = gate_start + part_id * f_cols + d * half_f + k * w
        return pltpu.make_async_copy(win_ref.at[:, pl.ds(pl.multiple_of(col, 128), w)],
                                     wgu.at[d, k, :, pl.ds(part_id * w, w)],
                                     wsem.at[(d * n_chunks + k) * 2 + part_id])

    def kv_copy(b, which):
        src, dst = ((kc_ref, kbuf), (vc_ref, vbuf))[which]
        return pltpu.make_async_copy(src.at[b], dst.at[b], kvsem.at[which, b])

    def wo_copy():
        return pltpu.make_async_copy(wout_ref, wo, wsem.at[4 * n_chunks + 1])

    wq_copy().start()

    @pl.loop(0, n_chunks)
    def _(k):
        for d in range(2):
            for s in range(2):
                wgu_copy(d, k, s).start()

    @pl.loop(0, seqs)
    def _(b):
        kv_copy(b, 0).start()
        kv_copy(b, 1).start()

    wo_copy().start()

    barrier = pltpu.get_barrier_semaphore()

    @pl.loop(1, group)
    def _(j):
        pl.semaphore_signal(barrier, inc=1, device_id=dev((me + j) % group), device_id_type=MESH)

    x_own = xs_ref[0:batch, :].astype(F32)
    s_own = jnp.sum(x_own, axis=1, keepdims=True)
    m2_own = jnp.sum(jnp.square(x_own - s_own * (1.0 / xw)), axis=1, keepdims=True)
    lane = lax.broadcasted_iota(jnp.int32, (batch, 128), 1)
    table = jnp.where(lane == 0, s_own, jnp.where(lane == 1, m2_own, 0.0))
    st[me] = table.T[0:8, :]

    pl.semaphore_wait(barrier, group - 1)

    def st_copy(slot, peer):
        return pltpu.make_async_remote_copy(st.at[slot], st.at[slot], st_s.at[peer], st_r.at[slot],
                                            device_id=dev(peer), device_id_type=MESH)

    def x_copy(slot, peer_c):
        return pltpu.make_async_remote_copy(xs_ref, xg.at[slot], xs_s.at[peer_c], xs_r.at[slot],
                                            device_id=(dp, r, peer_c), device_id_type=MESH)

    @pl.loop(1, group)
    def _(j):
        st_copy(me, (me + j) % group).start()

    @pl.loop(1, cols)
    def _(j):
        x_copy(c, (c + j) % cols).start()

    xg[c] = xs_ref[...]

    @pl.loop(1, group)
    def _(j):
        src = (me + j) % group
        st_copy(src, src).wait_recv()

    stats = st[...]
    sums = stats[:, 0:1, :]
    width = xw * group
    mean_row = jnp.sum(sums, axis=0) * (1.0 / width)
    dev_mean = sums * (1.0 / xw) - mean_row[None]
    m2_row = jnp.sum(stats[:, 1:2, :] + xw * jnp.square(dev_mean), axis=0)
    inv_row = lax.rsqrt(m2_row * (1.0 / width) + NORM_EPS)
    sub = lax.broadcasted_iota(jnp.int32, (128, batch), 0)
    back = jnp.where(sub == 0, mean_row, jnp.where(sub == 1, inv_row, 0.0)).T
    mean = back[:, 0:1]
    inv = back[:, 1:2]

    @pl.loop(1, cols)
    def _(j):
        src = (c + j) % cols
        x_copy(src, src).wait_recv()

    for cc in range(cols):
        xv = xg[cc, 0:batch, :].astype(F32)
        gain = xg[cc, batch:batch + GAIN_ROWS, :].astype(F32)[0:1, :]
        h[:, cc * xw:(cc + 1) * xw] = ((xv - mean) * inv * gain).astype(BF16)

    def q_copy(slot, peer):
        return pltpu.make_async_remote_copy(qsend.at[peer], qrecv.at[slot], q_s.at[peer], q_r.at[slot],
                                            device_id=dev(peer), device_id_type=MESH)

    wq_copy().wait()
    qkv = jnp.dot(h[...], wq[...], preferred_element_type=F32)
    qsend[...] = qkv.reshape(group, seqs, gate_start).astype(BF16)
    qrecv[me] = qsend[me]

    @pl.loop(1, group)
    def _(j):
        q_copy(me, (me + j) % group).start()

    acc[...] = jnp.zeros_like(acc)

    def rs_copy(d, k):
        nxt = (dp, r + 1, c) if d == 0 else (dp, r - 1, c)
        return pltpu.make_async_remote_copy(part.at[d, k], rbuf.at[d, k], rs_s.at[d, k], rs_r.at[d, k],
                                            device_id=nxt, device_id_type=MESH)

    def ag_copy(d, k):
        nxt = (dp, r - 1, c) if d == 0 else (dp, r + 1, c)
        return pltpu.make_async_remote_copy(mful.at[d, k], mful.at[d, k], ag_s.at[d, k], ag_r.at[d, k],
                                            device_id=nxt, device_id_type=MESH)

    pos = (r, rows - 1 - r)

    def partial_step(k):
        for d in range(2):
            wgu_copy(d, k, 0).wait()
            wgu_copy(d, k, 1).wait()
            part[d, k] = jnp.dot(h[...], wgu[d, k], preferred_element_type=F32).astype(BF16)

            @pl.when(pos[d] == 0)
            def _():
                rs_copy(d, k).start()

    def out_step(d, k):
        row0 = pl.multiple_of(q_cols + d * half_f + k * w, 128)
        acc[...] += jnp.dot(mful[d, k], wo[pl.ds(row0, w), :], preferred_element_type=F32)

    def reduce_step(d, k):
        total = part[d, k].astype(F32) + rbuf[d, k].astype(F32)

        @pl.when(pos[d] < rows - 1)
        def _():
            part[d, k] = total.astype(BF16)
            rs_copy(d, k).start()

        @pl.when(pos[d] == rows - 1)
        def _():
            full = total.astype(BF16).astype(F32)
            gate, up = full[:, :w], full[:, w:]
            mful[d, k] = (jax.nn.silu(gate) * up).astype(BF16)
            ag_copy(d, k).start()
            out_step(d, k)

    def prepare_queries():
        @pl.loop(1, group)
        def _(j):
            src = (me + j) % group
            q_copy(src, src).wait_recv()

        cos_t, sin_t = cos_ref[...], sin_ref[...]

        def rope(v):
            first, second = v[:, :128], v[:, 128:]
            return jnp.concatenate([first * cos_t - second * sin_t, second * cos_t + first * sin_t], axis=-1)

        k_parts, v_parts = [], []
        for cc in range(cols):
            full = qrecv[cc * rows].astype(F32)
            for rr in range(1, rows):
                full = full + qrecv[cc * rows + rr].astype(F32)
            full = full.astype(BF16).astype(F32)
            for i in range(heads_c):
                qhm[cc * heads_c + i] = rope(full[:, i * 256:(i + 1) * 256]) * (256 ** -0.5)
            k_parts.append(full[:, q_cols:q_cols + kv_cols])
            v_parts.append(full[:, q_cols + kv_cols:gate_start])
        k_row = rope(jnp.concatenate(k_parts, axis=-1)).astype(BF16)
        v_row = jnp.concatenate(v_parts, axis=-1).astype(BF16)
        knew_ref[...] = k_row
        vnew_ref[...] = v_row
        k_row, v_row = k_row.astype(F32), v_row.astype(F32)
        for b in range(seqs):
            qsm[b] = qhm[:, b, :].astype(BF16)
            kn3[b] = jnp.broadcast_to(k_row[b:b + 1, :], (8, 256))
            vn3[b] = jnp.broadcast_to(v_row[b:b + 1, :], (8, 256))

    def attend(b):
        kv_copy(b, 0).wait()
        kv_copy(b, 1).wait()
        q = qsm[b]
        limit = len_ref[b][0:1, 0:1]
        where_t = lax.broadcasted_iota(jnp.int32, (heads, cache_len), 1)
        scores = lax.dot_general(q, kbuf[b], (((1,), (1,)), ((), ())), preferred_element_type=F32)
        s_new = jnp.sum(q.astype(F32) * kn3[b][0:1, :], axis=1, keepdims=True)
        scores = jnp.where(where_t == limit, s_new, scores)
        scores = jnp.where(where_t <= limit, scores, -1e30)
        e = jnp.exp(scores - jnp.max(scores, axis=1, keepdims=True))
        probs = (e / jnp.sum(e, axis=1, keepdims=True)).astype(BF16).astype(F32)
        p_new = jnp.sum(jnp.where(where_t == limit, probs, 0.0), axis=1, keepdims=True)
        p_old = jnp.where(where_t == limit, 0.0, probs).astype(BF16)
        osm[b] = jnp.dot(p_old, vbuf[b], preferred_element_type=F32) + p_new * vn3[b][0:1, :]

    def at_copy(slot, peer):
        return pltpu.make_async_remote_copy(asend.at[peer // rows], arecv.at[slot], at_s.at[peer], at_r.at[slot],
                                            device_id=dev(peer), device_id_type=MESH)

    def send_attention():
        for cc in range(cols):
            asend[cc] = jnp.concatenate([osm[:, cc * heads_c + i, :] for i in range(heads_c)], axis=-1).astype(BF16)
        arecv[me] = asend[c]

        @pl.loop(1, group)
        def _(j):
            at_copy(me, (me + j) % group).start()

    @pl.loop(0, LEAD)
    def _(k):
        partial_step(k)

    first_attn = 3

    @pl.loop(0, n_chunks + 10)
    def _(i):
        @pl.when(i + LEAD < n_chunks)
        def _():
            partial_step(i + LEAD)

        for d in range(2):
            p = pos[d]
            k = i - (p + p // 2)

            @pl.when((p > 0) & (k >= 0) & (k < n_chunks))
            def _():
                rs_copy(d, k).wait_recv()
                reduce_step(d, k)

        for d in range(2):
            q = rows - 1 - pos[d]
            k = i - (5 + q + q // 2)

            @pl.when((q > 0) & (k >= 0) & (k < n_chunks))
            def _():
                ag_copy(d, k).wait_recv()

                @pl.when(q < rows - 1)
                def _():
                    ag_copy(d, k).start()

                out_step(d, k)

        @pl.when(i == first_attn - 1)
        def _():
            wo_copy().wait()
            prepare_queries()

        @pl.when((i >= first_attn) & (i < first_attn + seqs))
        def _():
            attend(i - first_attn)

        @pl.when(i == first_attn + seqs)
        def _():
            send_attention()

    @pl.loop(1, group)
    def _(j):
        src = (me + j) % group
        at_copy(src, src).wait_recv()

    attn = arecv[...].astype(F32).reshape(batch, q_cols).astype(BF16)
    total = (acc[...] + jnp.dot(attn, wo[0:q_cols, :], preferred_element_type=F32)).astype(BF16)
    for cc in range(cols):
        ysend[cc] = total[:, cc * xw:(cc + 1) * xw]

    def y_copy(slot, peer_c):
        return pltpu.make_async_remote_copy(ysend.at[peer_c], yrecv.at[slot], y_s.at[peer_c], y_r.at[slot],
                                            device_id=(dp, r, peer_c), device_id_type=MESH)

    @pl.loop(1, cols)
    def _(j):
        y_copy(c, (c + j) % cols).start()

    yrecv[c] = ysend[c]

    @pl.loop(1, group)
    def _(j):
        peer = (me + j) % group
        st_copy(me, peer).wait_send()
        q_copy(me, peer).wait_send()
        at_copy(me, peer).wait_send()

    @pl.loop(1, cols)
    def _(j):
        x_copy(c, (c + j) % cols).wait_send()

    @pl.loop(0, n_chunks)
    def _(k):
        for d in range(2):
            @pl.when(pos[d] < rows - 1)
            def _():
                rs_copy(d, k).wait_send()

            @pl.when(pos[d] > 0)
            def _():
                ag_copy(d, k).wait_send()

    @pl.loop(1, cols)
    def _(j):
        src = (c + j) % cols
        y_copy(src, src).wait_recv()

    delta = yrecv[0].astype(F32)
    for cc in range(1, cols):
        delta = delta + yrecv[cc].astype(F32)
    y_ref[...] = (xs_ref[0:batch, :].astype(F32) + delta.astype(BF16).astype(F32)).astype(BF16)

    @pl.loop(1, cols)
    def _(j):
        y_copy(c, (c + j) % cols).wait_send()


def solution(mesh):
    rows = mesh.shape['row']
    cols = mesh.shape['col']
    seq_spec = P(('dp', 'col', 'row'))
    act_spec = P('dp', ('row', 'col'))

    def local_layer(x, ln_gain, w_in, w_out, k_cache, v_cache, lengths, rope_cos, rope_sin):
        batch, xw = x.shape
        group = rows * cols
        seqs = batch // group
        head = rope_cos.shape[1] * 2
        cache_len = k_cache.shape[1]
        kdim, e_cols = w_in.shape
        r_cols, n_out = w_out.shape
        kv_cols = head // cols
        f_cols = e_cols - r_cols - 2 * kv_cols
        q_cols = r_cols - f_cols
        gate_start = q_cols + 2 * kv_cols
        heads = q_cols * cols // head
        w = CHUNK
        n_chunks = f_cols // 2 // w
        dims = (rows, cols, n_chunks, w, q_cols, kv_cols, f_cols)
        xs = jnp.concatenate([x, jnp.broadcast_to(ln_gain[None, :], (GAIN_ROWS, xw))], axis=0)
        len3 = jnp.broadcast_to(lengths[:, None, None], (seqs, 8, 128))
        vmem = pl.BlockSpec(memory_space=pltpu.VMEM)
        hbm = pl.BlockSpec(memory_space=pl.ANY)
        dma = pltpu.SemaphoreType.DMA
        y, k_new, v_new = pl.pallas_call(
            functools.partial(layer_kernel, dims),
            out_shape=(jax.ShapeDtypeStruct((batch, xw), BF16), jax.ShapeDtypeStruct((seqs, head), BF16),
                       jax.ShapeDtypeStruct((seqs, head), BF16)),
            in_specs=[vmem, hbm, hbm, hbm, hbm, vmem, vmem, vmem],
            out_specs=(vmem, vmem, vmem),
            scratch_shapes=[
                pltpu.VMEM((kdim, gate_start), BF16),
                pltpu.VMEM((2, n_chunks, kdim, 2 * w), BF16),
                pltpu.VMEM((r_cols, n_out), BF16),
                pltpu.VMEM((seqs, cache_len, head), BF16),
                pltpu.VMEM((seqs, cache_len, head), BF16),
                pltpu.VMEM((cols, batch + GAIN_ROWS, xw), BF16),
                pltpu.VMEM((group, 8, batch), F32),
                pltpu.VMEM((batch, kdim), BF16),
                pltpu.VMEM((2, n_chunks, batch, 2 * w), BF16),
                pltpu.VMEM((2, n_chunks, batch, 2 * w), BF16),
                pltpu.VMEM((2, n_chunks, batch, w), BF16),
                pltpu.VMEM((group, seqs, gate_start), BF16),
                pltpu.VMEM((group, seqs, gate_start), BF16),
                pltpu.VMEM((heads, seqs, head), F32),
                pltpu.VMEM((seqs, heads, head), BF16),
                pltpu.VMEM((seqs, 8, head), F32),
                pltpu.VMEM((seqs, 8, head), F32),
                pltpu.VMEM((seqs, heads, head), F32),
                pltpu.VMEM((cols, seqs, q_cols), BF16),
                pltpu.VMEM((group, seqs, q_cols), BF16),
                pltpu.VMEM((batch, n_out), F32),
                pltpu.VMEM((cols, batch, xw), BF16),
                pltpu.VMEM((cols, batch, xw), BF16),
                dma((4 * n_chunks + 2,)), dma((2, seqs)),
                dma((cols,)), dma((cols,)), dma((group,)), dma((group,)), dma((group,)), dma((group,)),
                dma((2, n_chunks)), dma((2, n_chunks)), dma((2, n_chunks)), dma((2, n_chunks)),
                dma((group,)), dma((group,)), dma((cols,)), dma((cols,)),
            ],
            compiler_params=pltpu.CompilerParams(collective_id=0, has_side_effects=True,
                                                 vmem_limit_bytes=62 * 1024 * 1024),
            name="layer",
        )(xs, w_in, w_out, k_cache, v_cache, len3, rope_cos, rope_sin)
        new_slot = (jnp.arange(cache_len)[None, :] == lengths[:, None])[:, :, None]
        k_out = jnp.where(new_slot, k_new[:, None, :], k_cache)
        v_out = jnp.where(new_slot, v_new[:, None, :], v_cache)
        return y, k_out, v_out

    return jax.shard_map(local_layer, mesh=mesh, in_specs=(act_spec, P(('row', 'col')), P('row', 'col'), P('col', 'row'), seq_spec, seq_spec, seq_spec, seq_spec, seq_spec), out_specs=(act_spec, seq_spec, seq_spec), check_vma=False)
```

time: 239 us -> 103 us (0.43)
  waiting for transfers between devices: 118 us -> 0 us
  Pallas kernels: 0 us -> 82.7 us
  blocking collectives: 54.6 us -> 0 us
  matrix products: 23.8 us -> 0 us
  between operations: 14.2 us -> 0.65 us
  starting transfers between devices: 6.65 us -> 0 us
  local copies, waits for them, and re-layouts: 6.08 us -> 2.64 us
    psum x1 -> x0, waiting for transfers between devices: 92.7 us -> none  [local_layer(): projected = lax.psum(part_in, 'row')]
    pallas_call x0 -> x1, Pallas kernels: none -> 82.7 us  [local_layer(): pl.pallas_call(functools.partial(layer_kernel, dims), out_shape=(jax.Shap...]
    psum x1 -> x0, blocking collectives: 35 us -> none  [local_layer(): row_stats = lax.psum(row_stats, ('row', 'col'))]
    dot_general x4 -> x0, matrix products: 23.8 us -> none  [the longest x1 10.6 us: local_layer(): jnp.dot(h_row, w_in, preferred_element_type=jnp.float32)]
    all_gather x2 -> x0, blocking collectives: 19.7 us -> none  [the longest x1 13.9 us: local_layer(): attn_rows = lax.all_gather(attn_parts, 'row', axis=1).reshape(batch, q_cols)]
    reduce_scatter x1 -> x0, waiting for transfers between devices: 18.6 us -> none  [local_layer(): delta = lax.psum_scatter(part_out, 'col', scatter_dimension=1, tiled=True)]
    all_to_all x2 -> x0, waiting for transfers between devices: 7 us -> none  [the longest x1 3.82 us: local_layer(): joined = lax.all_to_all(head_in, 'col', 0, 0, tiled=True).transpose(1, 0, 2)]
    all_to_all x2 -> x0, starting transfers between devices: 6.57 us -> none  [the longest x1 3.29 us: local_layer(): joined = lax.all_to_all(head_in, 'col', 0, 0, tiled=True).transpose(1, 0, 2)]
  transfers between devices with their start and end apart: 4 -> 0, of which waited for: 4 -> 0; matrix products, arithmetic and copies ran while one was open for 0% -> 0% of each run, Pallas kernels for 0% -> 0%
where the time goes in v1:
time: 103 us
  Pallas kernels  82.7 us (80%)
  other arithmetic  16.8 us (16%)
  local copies, waits for them, and re-layouts  2.64 us (3%)
    pallas_call x1, Pallas kernels, local_layer(): pl.pallas_call(functools.partial(layer_kernel, dims), out_shape=(jax.Shap...  82.7 us
    select_n x1, other arithmetic, local_layer(): v_out = jnp.where(new_slot, v_new[:, None, :], v_cache)  14.6 us

profile of v1, /device:TPU:0, one launch (start us, length us, event | category | flops | bytes accessed | tf_op | source)
XLA Modules:
  0.0 102.8 jit_solution(10868317435773914403)
XLA Ops:
  0.6 0.7 broadcast_in_dim.41
  1.3 0.7 iota_compare_fusion
  2.0 1.3 %broadcast_in_dim.42.len_ref = s32[8,8,128]{2,1,0:T(8,128)} broadcast(s32[8]{0:T(128)} %param.15), dimensions={0} | broadcast | bytes 32800 | tf_op jit(solution)/shard_map/broadcast_in_dim | solution.py:376
  3.4 1.5 %pad_maximum_fusion.xs_ref = bf16[144,256]{1,0:T(8,128)(2,1)} fusion(bf16[16,256]{1,0:T(8,128)(2,1)S(1)} %broadcast_in_dim.41, bf16[128,256]{1,0:T(8,128)(2,1)} %param.9), kind=kLoop, calls=%fused_computation.2 | loop fusion | flops 147456 | bytes 147456 | tf_op jit(solution)/shard_map/concatenate | solution.py:375
  4.8 82.7 %layer.1 = (bf16[128,256]{1,0:T(8,128)(2,1)}, bf16[8,256]{1,0:T(8,128)(2,1)}, bf16[8,256]{1,0:T(8,128)(2,1)}) custom-call(bf16[144,256]{1,0:T(8,128)(2,1)} %pad_maximum_fusion.xs_ref, bf16[1024,9344]{1,0:T(8,128)(2,1)} %win_ref.1, bf16[5120,1024]{1,0:T(8,128)(2,1)} %wout_ref.1, bf16[8,2048,256]{2,1,0:T(8,128)(2,1)} %kc_ref.1, bf16[8,2048,256]{2,1,0:T(8,128)(2,1)} %vc_ref.1, ...), custom_call_target="tpu_custom_call" | custom-call | tf_op jit(solution)/shard_map/layer/pallas_call | solution.py:380
  87.5 0.0 copy-start
  87.5 14.6 %broadcast_select_fusion = (bf16[8,2048,256]{2,1,0:T(8,128)(2,1)}, bf16[8,2048,256]{2,1,0:T(8,128)(2,1)}) fusion(bf16[8,2048,256]{2,1,0:T(8,128)(2,1)} %vc_ref.1, pred[8,2048]{1,0:T(8,128)(4,1)S(1)} %iota_compare_fusion, bf16[8,256]{1,0:T(8,128)(2,1)} %get-tuple-element.8, bf16[8,2048,256]{2,1,0:T(8,128)(2,1)} %kc_ref.1, bf16[8,256]{1,0:T(8,128)(2,1)} %get-tuple-element.7), kind=kLoop, calls=%fused_computation | loop fusion | flops 8388608 | bytes 33579008 | tf_op jit(solution)/shard_map/jit(_where)/select_n | solution.py:421
  102.1 0.0 copy-done
  102.1 0.6 copy.13
Async XLA Ops:
  87.5 14.6 %copy-start = (bf16[128,256]{1,0:T(8,128)(2,1)S(1)}, bf16[128,256]{1,0:T(8,128)(2,1)}, u32[]{:S(2)}) copy-start(bf16[128,256]{1,0:T(8,128)(2,1)} %get-tuple-element.14) | copy-start | bytes 196612

commit v2 on v1

--- a/solution.py
+++ b/solution.py
@@ -1,3 +1,4 @@
+import contextlib
 import functools
 
 import jax
@@ -12,15 +13,21 @@
 F32 = jnp.float32
 BF16 = jnp.bfloat16
 CHUNK = 128
-LEAD = 3
-GAIN_ROWS = 16
-
-
-def layer_kernel(dims, xs_ref, win_ref, wout_ref, kc_ref, vc_ref, len_ref, cos_ref, sin_ref,
-                 y_ref, knew_ref, vnew_ref,
-                 wq, wgu, wo, kbuf, vbuf, xg, st, h, part, rbuf, mful, qsend, qrecv, qhm, qsm, kn3, vn3, osm,
+ATTN_AT = 2
+SEND_AT = 10
+GATHER_AT = 15
+PROFILE = False
+
+
+def scope(name):
+    return jax.named_scope(name) if PROFILE else contextlib.nullcontext()
+
+
+def layer_kernel(dims, len_ref, x_ref, gain_ref, win_ref, wout_ref, kc_ref, vc_ref, cos_ref, sin_ref,
+                 y_ref, kbuf, vbuf,
+                 wq, wgu, wo, xg, gg, st, h, part, rbuf, mful, qsend, qrecv, qhm, qsm, kn3, vn3, osm,
                  asend, arecv, acc, ysend, yrecv,
-                 wsem, kvsem, xs_s, xs_r, st_s, st_r, q_s, q_r, rs_s, rs_r, ag_s, ag_r, at_s, at_r, y_s, y_r):
+                 wsem, kvsem, xs_s, xs_r, g_s, g_r, st_s, st_r, q_s, q_r, rs_s, rs_r, ag_s, ag_r, at_s, at_r, y_s, y_r):
     rows, cols, n_chunks, w, q_cols, kv_cols, f_cols = dims
     group = rows * cols
     dp, r, c = lax.axis_index("dp"), lax.axis_index("row"), lax.axis_index("col")
@@ -31,7 +38,7 @@
     half_f = f_cols // 2
     heads_c = q_cols // 256
     heads = heads_c * cols
-    cache_len = kbuf.shape[1]
+    cache_len, head = kbuf.shape[1:]
 
     def dev(g):
         return (dp, g % rows, g // rows)
@@ -42,7 +49,7 @@
     def wgu_copy(d, k, part_id):
         col = gate_start + part_id * f_cols + d * half_f + k * w
         return pltpu.make_async_copy(win_ref.at[:, pl.ds(pl.multiple_of(col, 128), w)],
-                                     wgu.at[d, k, :, pl.ds(part_id * w, w)],
+                                     wgu.at[k, :, pl.ds((2 * d + part_id) * w, w)],
                                      wsem.at[(d * n_chunks + k) * 2 + part_id])
 
     def kv_copy(b, which):
@@ -73,23 +80,29 @@
     def _(j):
         pl.semaphore_signal(barrier, inc=1, device_id=dev((me + j) % group), device_id_type=MESH)
 
-    x_own = xs_ref[0:batch, :].astype(F32)
+    x_own = x_ref[...].astype(F32)
     s_own = jnp.sum(x_own, axis=1, keepdims=True)
     m2_own = jnp.sum(jnp.square(x_own - s_own * (1.0 / xw)), axis=1, keepdims=True)
     lane = lax.broadcasted_iota(jnp.int32, (batch, 128), 1)
     table = jnp.where(lane == 0, s_own, jnp.where(lane == 1, m2_own, 0.0))
     st[me] = table.T[0:8, :]
-
-    pl.semaphore_wait(barrier, group - 1)
+    gg[c] = jnp.broadcast_to(gain_ref[...].astype(F32), (8, xw))
+
+    with scope('barrier'):
+        pl.semaphore_wait(barrier, group - 1)
 
     def st_copy(slot, peer):
         return pltpu.make_async_remote_copy(st.at[slot], st.at[slot], st_s.at[peer], st_r.at[slot],
                                             device_id=dev(peer), device_id_type=MESH)
 
     def x_copy(slot, peer_c):
-        return pltpu.make_async_remote_copy(xs_ref, xg.at[slot], xs_s.at[peer_c], xs_r.at[slot],
+        return pltpu.make_async_remote_copy(x_ref, xg.at[slot], xs_s.at[peer_c], xs_r.at[slot],
                                             device_id=(dp, r, peer_c), device_id_type=MESH)
 
+    def g_copy(slot, peer_c):
+        return pltpu.make_async_remote_copy(gg.at[slot], gg.at[slot], g_s.at[peer_c], g_r.at[slot],
+                                            device_id=(dp, r, peer_c), device_id_type=MESH)
+
     @pl.loop(1, group)
     def _(j):
         st_copy(me, (me + j) % group).start()
@@ -97,13 +110,15 @@
     @pl.loop(1, cols)
     def _(j):
         x_copy(c, (c + j) % cols).start()
-
-    xg[c] = xs_ref[...]
+        g_copy(c, (c + j) % cols).start()
+
+    xg[c] = x_ref[...]
 
     @pl.loop(1, group)
     def _(j):
         src = (me + j) % group
-        st_copy(src, src).wait_recv()
+        with scope('stats'):
+            st_copy(src, src).wait_recv()
 
     stats = st[...]
     sums = stats[:, 0:1, :]
@@ -120,18 +135,21 @@
     @pl.loop(1, cols)
     def _(j):
         src = (c + j) % cols
-        x_copy(src, src).wait_recv()
+        with scope('xwait'):
+            x_copy(src, src).wait_recv()
+            g_copy(src, src).wait_recv()
 
     for cc in range(cols):
-        xv = xg[cc, 0:batch, :].astype(F32)
-        gain = xg[cc, batch:batch + GAIN_ROWS, :].astype(F32)[0:1, :]
+        xv = xg[cc].astype(F32)
+        gain = gg[cc, 0:1, :]
         h[:, cc * xw:(cc + 1) * xw] = ((xv - mean) * inv * gain).astype(BF16)
 
     def q_copy(slot, peer):
         return pltpu.make_async_remote_copy(qsend.at[peer], qrecv.at[slot], q_s.at[peer], q_r.at[slot],
                                             device_id=dev(peer), device_id_type=MESH)
 
-    wq_copy().wait()
+    with scope('wqwait'):
+        wq_copy().wait()
     qkv = jnp.dot(h[...], wq[...], preferred_element_type=F32)
     qsend[...] = qkv.reshape(group, seqs, gate_start).astype(BF16)
     qrecv[me] = qsend[me]
@@ -158,7 +176,9 @@
         for d in range(2):
             wgu_copy(d, k, 0).wait()
             wgu_copy(d, k, 1).wait()
-            part[d, k] = jnp.dot(h[...], wgu[d, k], preferred_element_type=F32).astype(BF16)
+        both = jnp.dot(h[...], wgu[k], preferred_element_type=F32).astype(BF16)
+        for d in range(2):
+            part[d, k] = both[:, d * 2 * w:(d + 1) * 2 * w]
 
             @pl.when(pos[d] == 0)
             def _():
@@ -208,8 +228,6 @@
             v_parts.append(full[:, q_cols + kv_cols:gate_start])
         k_row = rope(jnp.concatenate(k_parts, axis=-1)).astype(BF16)
         v_row = jnp.concatenate(v_parts, axis=-1).astype(BF16)
-        knew_ref[...] = k_row
-        vnew_ref[...] = v_row
         k_row, v_row = k_row.astype(F32), v_row.astype(F32)
         for b in range(seqs):
             qsm[b] = qhm[:, b, :].astype(BF16)
@@ -219,18 +237,18 @@
     def attend(b):
         kv_copy(b, 0).wait()
         kv_copy(b, 1).wait()
-        q = qsm[b]
-        limit = len_ref[b][0:1, 0:1]
+        limit = len_ref[b]
+        slot = lax.broadcasted_iota(jnp.int32, (cache_len, head), 0) == limit
+        k_all = jnp.where(slot, kn3[b][0:1, :].astype(BF16), kbuf[b])
+        v_all = jnp.where(slot, vn3[b][0:1, :].astype(BF16), vbuf[b])
+        kbuf[b] = k_all
+        vbuf[b] = v_all
+        scores = lax.dot_general(qsm[b], k_all, (((1,), (1,)), ((), ())), preferred_element_type=F32)
         where_t = lax.broadcasted_iota(jnp.int32, (heads, cache_len), 1)
-        scores = lax.dot_general(q, kbuf[b], (((1,), (1,)), ((), ())), preferred_element_type=F32)
-        s_new = jnp.sum(q.astype(F32) * kn3[b][0:1, :], axis=1, keepdims=True)
-        scores = jnp.where(where_t == limit, s_new, scores)
         scores = jnp.where(where_t <= limit, scores, -1e30)
         e = jnp.exp(scores - jnp.max(scores, axis=1, keepdims=True))
-        probs = (e / jnp.sum(e, axis=1, keepdims=True)).astype(BF16).astype(F32)
-        p_new = jnp.sum(jnp.where(where_t == limit, probs, 0.0), axis=1, keepdims=True)
-        p_old = jnp.where(where_t == limit, 0.0, probs).astype(BF16)
-        osm[b] = jnp.dot(p_old, vbuf[b], preferred_element_type=F32) + p_new * vn3[b][0:1, :]
+        probs = (e / jnp.sum(e, axis=1, keepdims=True)).astype(BF16)
+        osm[b] = jnp.dot(probs, v_all, preferred_element_type=F32)
 
     def at_copy(slot, peer):
         return pltpu.make_async_remote_copy(asend.at[peer // rows], arecv.at[slot], at_s.at[peer], at_r.at[slot],
@@ -245,63 +263,68 @@
         def _(j):
             at_copy(me, (me + j) % group).start()
 
-    @pl.loop(0, LEAD)
+    @pl.loop(0, n_chunks)
     def _(k):
-        partial_step(k)
-
-    first_attn = 3
-
-    @pl.loop(0, n_chunks + 10)
+        with scope('partial'):
+            partial_step(k)
+
+    @pl.loop(0, GATHER_AT + 2 * (rows - 2) + n_chunks // 2)
     def _(i):
-        @pl.when(i + LEAD < n_chunks)
-        def _():
-            partial_step(i + LEAD)
-
         for d in range(2):
             p = pos[d]
-            k = i - (p + p // 2)
+            k = i - 2 * (p - 1)
 
             @pl.when((p > 0) & (k >= 0) & (k < n_chunks))
             def _():
-                rs_copy(d, k).wait_recv()
-                reduce_step(d, k)
+                with scope('rswait%d' % d):
+                    rs_copy(d, k).wait_recv()
+                with scope('reduce%d' % d):
+                    reduce_step(d, k)
 
         for d in range(2):
             q = rows - 1 - pos[d]
-            k = i - (5 + q + q // 2)
-
-            @pl.when((q > 0) & (k >= 0) & (k < n_chunks))
+            k2 = i - GATHER_AT - 2 * (q - 1)
+
+            @pl.when((q > 0) & (k2 >= 0) & (k2 < n_chunks // 2))
             def _():
-                ag_copy(d, k).wait_recv()
-
-                @pl.when(q < rows - 1)
-                def _():
-                    ag_copy(d, k).start()
-
-                out_step(d, k)
-
-        @pl.when(i == first_attn - 1)
+                for k in (2 * k2, 2 * k2 + 1):
+                    with scope('agwait%d' % d):
+                        ag_copy(d, k).wait_recv()
+
+                    @pl.when(q < rows - 1)
+                    def _():
+                        ag_copy(d, k).start()
+
+                    with scope('outstep'):
+                        out_step(d, k)
+
+        @pl.when(i == ATTN_AT - 1)
         def _():
-            wo_copy().wait()
-            prepare_queries()
-
-        @pl.when((i >= first_attn) & (i < first_attn + seqs))
+            with scope('prepare'):
+                wo_copy().wait()
+                prepare_queries()
+
+        @pl.when((i >= ATTN_AT) & (i < ATTN_AT + seqs))
         def _():
-            attend(i - first_attn)
-
-        @pl.when(i == first_attn + seqs)
+            with scope('attend'):
+                attend(i - ATTN_AT)
+
+        @pl.when(i == SEND_AT)
         def _():
-            send_attention()
+            with scope('sendattn'):
+                send_attention()
 
     @pl.loop(1, group)
     def _(j):
         src = (me + j) % group
-        at_copy(src, src).wait_recv()
-
-    attn = arecv[...].astype(F32).reshape(batch, q_cols).astype(BF16)
-    total = (acc[...] + jnp.dot(attn, wo[0:q_cols, :], preferred_element_type=F32)).astype(BF16)
-    for cc in range(cols):
-        ysend[cc] = total[:, cc * xw:(cc + 1) * xw]
+        with scope('atwait'):
+            at_copy(src, src).wait_recv()
+
+    with scope('final'):
+        attn = arecv[...].astype(F32).reshape(batch, q_cols).astype(BF16)
+        total = (acc[...] + jnp.dot(attn, wo[0:q_cols, :], preferred_element_type=F32)).astype(BF16)
+        for cc in range(cols):
+            ysend[cc] = total[:, cc * xw:(cc + 1) * xw]
 
     def y_copy(slot, peer_c):
         return pltpu.make_async_remote_copy(ysend.at[peer_c], yrecv.at[slot], y_s.at[peer_c], y_r.at[slot],
@@ -323,6 +346,7 @@
     @pl.loop(1, cols)
     def _(j):
         x_copy(c, (c + j) % cols).wait_send()
+        g_copy(c, (c + j) % cols).wait_send()
 
     @pl.loop(0, n_chunks)
     def _(k):
@@ -338,16 +362,19 @@
     @pl.loop(1, cols)
     def _(j):
         src = (c + j) % cols
-        y_copy(src, src).wait_recv()
-
-    delta = yrecv[0].astype(F32)
-    for cc in range(1, cols):
-        delta = delta + yrecv[cc].astype(F32)
-    y_ref[...] = (xs_ref[0:batch, :].astype(F32) + delta.astype(BF16).astype(F32)).astype(BF16)
-
-    @pl.loop(1, cols)
-    def _(j):
-        y_copy(c, (c + j) % cols).wait_send()
+        with scope('ywait'):
+            y_copy(src, src).wait_recv()
+
+    with scope('yout'):
+        delta = yrecv[0].astype(F32)
+        for cc in range(1, cols):
+            delta = delta + yrecv[cc].astype(F32)
+        y_ref[...] = (x_ref[...].astype(F32) + delta.astype(BF16).astype(F32)).astype(BF16)
+
+    @pl.loop(1, cols)
+    def _(j):
+        with scope('ysent'):
+            y_copy(c, (c + j) % cols).wait_send()
 
 
 def solution(mesh):
@@ -372,24 +399,21 @@
         w = CHUNK
         n_chunks = f_cols // 2 // w
         dims = (rows, cols, n_chunks, w, q_cols, kv_cols, f_cols)
-        xs = jnp.concatenate([x, jnp.broadcast_to(ln_gain[None, :], (GAIN_ROWS, xw))], axis=0)
-        len3 = jnp.broadcast_to(lengths[:, None, None], (seqs, 8, 128))
         vmem = pl.BlockSpec(memory_space=pltpu.VMEM)
         hbm = pl.BlockSpec(memory_space=pl.ANY)
         dma = pltpu.SemaphoreType.DMA
-        y, k_new, v_new = pl.pallas_call(
+        return pl.pallas_call(
             functools.partial(layer_kernel, dims),
-            out_shape=(jax.ShapeDtypeStruct((batch, xw), BF16), jax.ShapeDtypeStruct((seqs, head), BF16),
-                       jax.ShapeDtypeStruct((seqs, head), BF16)),
-            in_specs=[vmem, hbm, hbm, hbm, hbm, vmem, vmem, vmem],
+            out_shape=(jax.ShapeDtypeStruct((batch, xw), BF16), pltpu.VMEM((seqs, cache_len, head), BF16),
+                       pltpu.VMEM((seqs, cache_len, head), BF16)),
+            in_specs=[pl.BlockSpec(memory_space=pltpu.SMEM), vmem, vmem, hbm, hbm, hbm, hbm, vmem, vmem],
             out_specs=(vmem, vmem, vmem),
             scratch_shapes=[
                 pltpu.VMEM((kdim, gate_start), BF16),
-                pltpu.VMEM((2, n_chunks, kdim, 2 * w), BF16),
+                pltpu.VMEM((n_chunks, kdim, 4 * w), BF16),
                 pltpu.VMEM((r_cols, n_out), BF16),
-                pltpu.VMEM((seqs, cache_len, head), BF16),
-                pltpu.VMEM((seqs, cache_len, head), BF16),
-                pltpu.VMEM((cols, batch + GAIN_ROWS, xw), BF16),
+                pltpu.VMEM((cols, batch, xw), BF16),
+                pltpu.VMEM((cols, 8, xw), F32),
                 pltpu.VMEM((group, 8, batch), F32),
                 pltpu.VMEM((batch, kdim), BF16),
                 pltpu.VMEM((2, n_chunks, batch, 2 * w), BF16),
@@ -408,17 +432,14 @@
                 pltpu.VMEM((cols, batch, xw), BF16),
                 pltpu.VMEM((cols, batch, xw), BF16),
                 dma((4 * n_chunks + 2,)), dma((2, seqs)),
-                dma((cols,)), dma((cols,)), dma((group,)), dma((group,)), dma((group,)), dma((group,)),
+                dma((cols,)), dma((cols,)), dma((cols,)), dma((cols,)),
+                dma((group,)), dma((group,)), dma((group,)), dma((group,)),
                 dma((2, n_chunks)), dma((2, n_chunks)), dma((2, n_chunks)), dma((2, n_chunks)),
                 dma((group,)), dma((group,)), dma((cols,)), dma((cols,)),
             ],
             compiler_params=pltpu.CompilerParams(collective_id=0, has_side_effects=True,
-                                                 vmem_limit_bytes=62 * 1024 * 1024),
+                                                 vmem_limit_bytes=44 * 1024 * 1024),
             name="layer",
-        )(xs, w_in, w_out, k_cache, v_cache, len3, rope_cos, rope_sin)
-        new_slot = (jnp.arange(cache_len)[None, :] == lengths[:, None])[:, :, None]
-        k_out = jnp.where(new_slot, k_new[:, None, :], k_cache)
-        v_out = jnp.where(new_slot, v_new[:, None, :], v_cache)
-        return y, k_out, v_out
+        )(lengths, x, ln_gain[None, :], w_in, w_out, k_cache, v_cache, rope_cos, rope_sin)
 
     return jax.shard_map(local_layer, mesh=mesh, in_specs=(act_spec, P(('row', 'col')), P('row', 'col'), P('col', 'row'), seq_spec, seq_spec, seq_spec, seq_spec, seq_spec), out_specs=(act_spec, seq_spec, seq_spec), check_vma=False)

time: 103 us -> 86 us (0.83)
  other arithmetic: 16.8 us -> 0 us
  Pallas kernels: 82.7 us -> 76.6 us
  local copies, waits for them, and re-layouts: 2.64 us -> 8.65 us
    select_n x1 -> x0, other arithmetic: 14.6 us -> none  [local_layer(): v_out = jnp.where(new_slot, v_new[:, None, :], v_cache)]
    unnamed x3 -> x5, local copies, waits for them, and re-layouts: 0.63 us -> 7.43 us
    pallas_call x1, Pallas kernels: 82.7 us -> 76.6 us  [local_layer(): pl.pallas_call(functools.partial(layer_kernel, dims), out_shape=(jax.Shap...]
    concatenate x1 -> x0, other arithmetic: 1.48 us -> none  [local_layer(): jnp.concatenate([x, jnp.broadcast_to(ln_gain[None, :], (GAIN_ROWS, xw))],...]
where the time goes in v2:
time: 86 us; the launch traced here: 85.9 us
  Pallas kernels  76.6 us (89%)
  local copies, waits for them, and re-layouts  8.65 us (10%)
    pallas_call x1, Pallas kernels, local_layer(): pl.pallas_call(functools.partial(layer_kernel, dims), out_shape=(jax.Shap...  76.6 us
    unnamed x5, local copies, waits for them, and re-layouts  7.43 us

profile of v2, /device:TPU:0, one launch (start us, length us, event | category | flops | bytes accessed | tf_op | source)
XLA Modules:
  0.0 85.9 jit_solution(6761720078179106173)
XLA Ops:
  0.6 1.2 %broadcast_in_dim.3.gain_ref = bf16[1,256]{1,0:T(2,128)(2,1)} reshape(bf16[256]{0:T(256)(128)(2,1)} %param.10) | data formatting | bytes 1024 | tf_op jit(solution)/shard_map/broadcast_in_dim | solution.py:443
  1.9 76.6 %layer.1 = (bf16[128,256]{1,0:T(8,128)(2,1)}, bf16[8,2048,256]{2,1,0:T(8,128)(2,1)S(1)}, bf16[8,2048,256]{2,1,0:T(8,128)(2,1)S(1)}) custom-call(s32[8]{0:T(128)} %len_ref.1, bf16[128,256]{1,0:T(8,128)(2,1)} %x_ref.1, bf16[1,256]{1,0:T(2,128)(2,1)} %broadcast_in_dim.3.gain_ref, bf16[1024,9344]{1,0:T(8,128)(2,1)} %win_ref.1, bf16[5120,1024]{1,0:T(8,128)(2,1)} %wout_ref.1, ...), custom_call_target="tpu_custom_call" | custom-call | tf_op jit(solution)/shard_map/layer/pallas_call | solution.py:405
  78.4 3.4 %copy.15 = bf16[8,2048,256]{2,1,0:T(8,128)(2,1)} copy(bf16[8,2048,256]{2,1,0:T(8,128)(2,1)S(1)} %get-tuple-element.4) | data formatting | bytes 16777216
  81.8 0.0 copy-start
  81.8 3.4 %copy.16 = bf16[8,2048,256]{2,1,0:T(8,128)(2,1)} copy(bf16[8,2048,256]{2,1,0:T(8,128)(2,1)S(1)} %get-tuple-element.5) | data formatting | bytes 16777216
  85.2 0.0 copy-done
  85.2 0.6 copy.17
Async XLA Ops:
  81.8 3.4 %copy-start = (bf16[128,256]{1,0:T(8,128)(2,1)S(1)}, bf16[128,256]{1,0:T(8,128)(2,1)}, u32[]{:S(2)}) copy-start(bf16[128,256]{1,0:T(8,128)(2,1)} %get-tuple-element.9) | copy-start | bytes 196612

commit v3 on v2

v3 whole, which is shorter than its diff:
```python
import contextlib
import functools

import jax
import jax.numpy as jnp
from jax import lax
from jax.experimental import pallas as pl
from jax.experimental.pallas import tpu as pltpu
from jax.sharding import PartitionSpec as P

NORM_EPS = 1e-6
MESH = pl.DeviceIdType.MESH
F32 = jnp.float32
BF16 = jnp.bfloat16
CHUNK = 128
FIRST = 4
BEFORE = 8
LAG = 3
ATTN_AT = 7
SEND_AT = 18
GATHER_AT = 15
GATHER_LAG = 3
PROFILE = False


def scope(name):
    return jax.named_scope(name) if PROFILE else contextlib.nullcontext()


def layer_kernel(dims, len_hbm, x_hbm, gain_hbm, win_ref, wout_ref, kc_ref, vc_ref, cos_hbm, sin_hbm,
                 y_refs, kbuf, vbuf,
                 len_ref, gain_ref, cos_ref, sin_ref, wq, wgu, wo, xg, gg, st, h, part, rbuf, mful, qsend, qrecv, qhm, qsm, kn3, vn3, osm,
                 asend, arecv, acc, total_ref,
                 isem, wsem, kvsem, xs_s, xs_r, g_s, g_r, st_s, st_r, q_s, q_r, rs_s, rs_r, ag_s, ag_r, at_s, at_r):
    rows, cols, n_chunks, w, q_cols, kv_cols, f_cols = dims
    group = rows * cols
    dp, r, c = lax.axis_index("dp"), lax.axis_index("row"), lax.axis_index("col")
    me = c * rows + r
    batch, xw = y_refs[0].shape
    seqs = batch // group
    gate_start = q_cols + 2 * kv_cols
    half_f = f_cols // 2
    heads_c = q_cols // 256
    heads = heads_c * cols
    cache_len, head = kbuf.shape[1:]

    def dev(g):
        return (dp, g % rows, g // rows)

    small = [pltpu.make_async_copy(src, dst, isem.at[i]) for i, (src, dst) in enumerate(
        ((x_hbm, xg.at[c]), (gain_hbm, gain_ref), (cos_hbm, cos_ref), (sin_hbm, sin_ref), (len_hbm, len_ref)))]
    for copy in small:
        copy.start()

    barrier = pltpu.get_barrier_semaphore()

    @pl.loop(1, group)
    def _(j):
        pl.semaphore_signal(barrier, inc=1, device_id=dev((me + j) % group), device_id_type=MESH)

    def wq_copy():
        return pltpu.make_async_copy(win_ref.at[:, pl.ds(0, gate_start)], wq, wsem.at[n_chunks])

    def wgu_copy(d, k, part_id):
        col = gate_start + part_id * f_cols + d * half_f + k * w
        return pltpu.make_async_copy(win_ref.at[:, pl.ds(pl.multiple_of(col, 128), w)],
                                     wgu.at[k, :, pl.ds((2 * d + part_id) * w, w)],
                                     wsem.at[k])

    def kv_copy(b, which):
        src, dst = ((kc_ref, kbuf), (vc_ref, vbuf))[which]
        return pltpu.make_async_copy(src.at[b], dst.at[b], kvsem.at[b])

    def wo_copy():
        return pltpu.make_async_copy(wout_ref, wo, wsem.at[n_chunks + 1])

    wq_copy().start()

    @pl.loop(0, n_chunks)
    def _(k):
        for d in range(2):
            for s in range(2):
                wgu_copy(d, k, s).start()

    @pl.loop(0, seqs)
    def _(b):
        kv_copy(b, 0).start()
        kv_copy(b, 1).start()

    wo_copy().start()

    def all_bytes(ref, n, send_sem, recv_sem):
        part_ref = ref.at[pl.ds(0, n)]
        return pltpu.make_async_remote_copy(part_ref, part_ref, send_sem, recv_sem,
                                            device_id=dev((me + 1) % group), device_id_type=MESH)

    small[0].wait()
    small[1].wait()
    x_own = xg[c].astype(F32)
    s_own = jnp.sum(x_own, axis=1, keepdims=True)
    m2_own = jnp.sum(jnp.square(x_own - s_own * (1.0 / xw)), axis=1, keepdims=True)
    lane = lax.broadcasted_iota(jnp.int32, (batch, 128), 1)
    table = jnp.where(lane == 0, s_own, jnp.where(lane == 1, m2_own, 0.0))
    st[me] = table.T[0:8, :]
    gg[c] = jnp.broadcast_to(gain_ref[...].astype(F32).reshape(1, xw), (8, xw))

    with scope('barrier'):
        pl.semaphore_wait(barrier, group - 1)

    def st_copy(slot, peer):
        return pltpu.make_async_remote_copy(st.at[slot], st.at[slot], st_s, st_r,
                                            device_id=dev(peer), device_id_type=MESH)

    def x_copy(slot, peer_c):
        return pltpu.make_async_remote_copy(xg.at[slot], xg.at[slot], xs_s, xs_r,
                                            device_id=(dp, r, peer_c), device_id_type=MESH)

    def g_copy(slot, peer_c):
        return pltpu.make_async_remote_copy(gg.at[slot], gg.at[slot], g_s, g_r,
                                            device_id=(dp, r, peer_c), device_id_type=MESH)

    @pl.loop(1, group)
    def _(j):
        st_copy(me, (me + j) % group).start()

    @pl.loop(1, cols)
    def _(j):
        x_copy(c, (c + j) % cols).start()
        g_copy(c, (c + j) % cols).start()


    with scope('stats'):
        all_bytes(st, group - 1, st_s, st_r).wait_recv()

    stats = st[...]
    sums = stats[:, 0:1, :]
    width = xw * group
    mean_row = jnp.sum(sums, axis=0) * (1.0 / width)
    dev_mean = sums * (1.0 / xw) - mean_row[None]
    m2_row = jnp.sum(stats[:, 1:2, :] + xw * jnp.square(dev_mean), axis=0)
    inv_row = lax.rsqrt(m2_row * (1.0 / width) + NORM_EPS)
    sub = lax.broadcasted_iota(jnp.int32, (128, batch), 0)
    back = jnp.where(sub == 0, mean_row, jnp.where(sub == 1, inv_row, 0.0)).T
    mean = back[:, 0:1]
    inv = back[:, 1:2]

    with scope('xwait'):
        all_bytes(xg, cols - 1, xs_s, xs_r).wait_recv()
        all_bytes(gg, cols - 1, g_s, g_r).wait_recv()

    for cc in range(cols):
        xv = xg[cc].astype(F32)
        gain = gg[cc, 0:1, :]
        h[:, cc * xw:(cc + 1) * xw] = ((xv - mean) * inv * gain).astype(BF16)

    acc[...] = jnp.zeros_like(acc)

    def rs_copy(d, k):
        nxt = (dp, r + 1, c) if d == 0 else (dp, r - 1, c)
        return pltpu.make_async_remote_copy(part.at[d, k], rbuf.at[d, k], rs_s.at[d], rs_r.at[d, k],
                                            device_id=nxt, device_id_type=MESH)

    def ag_copy(d, k):
        nxt = (dp, r - 1, c) if d == 0 else (dp, r + 1, c)
        return pltpu.make_async_remote_copy(mful.at[d, k], mful.at[d, k], ag_s.at[d], ag_r.at[d, k],
                                            device_id=nxt, device_id_type=MESH)

    pos = (r, rows - 1 - r)

    def partial_step(k):
        pltpu.make_async_copy(win_ref.at[:, pl.ds(0, 4 * w)], wgu.at[k], wsem.at[k]).wait()
        both = jnp.dot(h[...], wgu[k], preferred_element_type=F32).astype(BF16)
        for d in range(2):
            part[d, k] = both[:, d * 2 * w:(d + 1) * 2 * w]

            @pl.when(pos[d] == 0)
            def _():
                rs_copy(d, k).start()

    def out_step(d, k):
        row0 = pl.multiple_of(q_cols + d * half_f + k * w, 128)
        acc[...] += jnp.dot(mful[d, k], wo[pl.ds(row0, w), :], preferred_element_type=F32)

    def reduce_step(d, k):
        total = part[d, k].astype(F32) + rbuf[d, k].astype(F32)

        @pl.when(pos[d] < rows - 1)
        def _():
            part[d, k] = total.astype(BF16)
            rs_copy(d, k).start()

        @pl.when(pos[d] == rows - 1)
        def _():
            full = total.astype(BF16).astype(F32)
            gate, up = full[:, :w], full[:, w:]
            mful[d, k] = (jax.nn.silu(gate) * up).astype(BF16)
            ag_copy(d, k).start()
            out_step(d, k)

    def prepare_queries():
        all_bytes(qrecv, group - 1, q_s, q_r).wait_recv()

        cos_t, sin_t = cos_ref[...], sin_ref[...]

        def rope(v):
            first, second = v[:, :128], v[:, 128:]
            return jnp.concatenate([first * cos_t - second * sin_t, second * cos_t + first * sin_t], axis=-1)

        k_parts, v_parts = [], []
        for cc in range(cols):
            full = qrecv[cc * rows].astype(F32)
            for rr in range(1, rows):
                full = full + qrecv[cc * rows + rr].astype(F32)
            full = full.astype(BF16).astype(F32)
            for i in range(heads_c):
                qhm[cc * heads_c + i] = rope(full[:, i * 256:(i + 1) * 256]) * (256 ** -0.5)
            k_parts.append(full[:, q_cols:q_cols + kv_cols])
            v_parts.append(full[:, q_cols + kv_cols:gate_start])
        k_row = rope(jnp.concatenate(k_parts, axis=-1)).astype(BF16)
        v_row = jnp.concatenate(v_parts, axis=-1).astype(BF16)
        k_row, v_row = k_row.astype(F32), v_row.astype(F32)
        for b in range(seqs):
            qsm[b] = qhm[:, b, :].astype(BF16)
            kn3[b] = jnp.broadcast_to(k_row[b:b + 1, :], (8, 256))
            vn3[b] = jnp.broadcast_to(v_row[b:b + 1, :], (8, 256))

    def attend(b):
        pltpu.make_async_copy(kc_ref.at[pl.ds(0, 2)], kbuf.at[pl.ds(0, 2)], kvsem.at[b]).wait()
        limit = len_ref[b]
        slot = lax.broadcasted_iota(jnp.int32, (cache_len, head), 0) == limit
        k_all = jnp.where(slot, kn3[b][0:1, :].astype(BF16), kbuf[b])
        v_all = jnp.where(slot, vn3[b][0:1, :].astype(BF16), vbuf[b])
        kbuf[b] = k_all
        vbuf[b] = v_all
        scores = lax.dot_general(qsm[b], k_all, (((1,), (1,)), ((), ())), preferred_element_type=F32)
        where_t = lax.broadcasted_iota(jnp.int32, (heads, cache_len), 1)
        scores = jnp.where(where_t <= limit, scores, -1e30)
        e = jnp.exp(scores - jnp.max(scores, axis=1, keepdims=True))
        probs = (e / jnp.sum(e, axis=1, keepdims=True)).astype(BF16)
        osm[b] = jnp.dot(probs, v_all, preferred_element_type=F32)

    def at_copy(slot, peer):
        return pltpu.make_async_remote_copy(asend.at[peer // rows], arecv.at[slot], at_s, at_r,
                                            device_id=dev(peer), device_id_type=MESH)

    def send_attention():
        for cc in range(cols):
            asend[cc] = jnp.concatenate([osm[:, cc * heads_c + i, :] for i in range(heads_c)], axis=-1).astype(BF16)
        arecv[me] = asend[c]

        @pl.loop(1, group)
        def _(j):
            at_copy(me, (me + j) % group).start()

    @pl.loop(0, FIRST)
    def _(k):
        with scope('partial'):
            partial_step(k)

    def q_copy(slot, peer):
        return pltpu.make_async_remote_copy(qsend.at[peer], qrecv.at[slot], q_s, q_r,
                                            device_id=dev(peer), device_id_type=MESH)

    with scope('wqwait'):
        wq_copy().wait()
    qkv = jnp.dot(h[...], wq[...], preferred_element_type=F32)
    qsend[...] = qkv.reshape(group, seqs, gate_start).astype(BF16)
    qrecv[me] = qsend[me]

    @pl.loop(1, group)
    def _(j):
        q_copy(me, (me + j) % group).start()

    @pl.loop(FIRST, BEFORE)
    def _(k):
        with scope('partial'):
            partial_step(k)

    @pl.loop(0, max(GATHER_AT + GATHER_LAG * (rows - 2) + n_chunks // 2, LAG * (rows - 2) + n_chunks))
    def _(i):
        @pl.when(i == LAG)
        def _():
            wo_copy().wait()

        for half in range(2):
            @pl.when(BEFORE + 2 * i + half < n_chunks)
            def _():
                with scope('partial'):
                    partial_step(BEFORE + 2 * i + half)

        for d in range(2):
            p = pos[d]
            k = i - LAG * (p - 1)

            @pl.when((p > 0) & (k >= 0) & (k < n_chunks))
            def _():
                with scope('rswait%d' % d):
                    rs_copy(d, k).wait_recv()
                with scope('reduce%d' % d):
                    reduce_step(d, k)

        for d in range(2):
            q = rows - 1 - pos[d]
            k2 = i - GATHER_AT - GATHER_LAG * (q - 1)

            @pl.when((q > 0) & (k2 >= 0) & (k2 < n_chunks // 2))
            def _():
                for k in (2 * k2, 2 * k2 + 1):
                    with scope('agwait%d' % d):
                        ag_copy(d, k).wait_recv()

                    @pl.when(q < rows - 1)
                    def _():
                        ag_copy(d, k).start()

                    with scope('outstep'):
                        out_step(d, k)

        @pl.when(i == ATTN_AT - 1)
        def _():
            with scope('prepare'):
                for copy in small[2:]:
                    copy.wait()
                prepare_queries()

        @pl.when((i >= ATTN_AT) & (i < ATTN_AT + seqs))
        def _():
            with scope('attend'):
                attend(i - ATTN_AT)

        @pl.when(i == SEND_AT)
        def _():
            with scope('sendattn'):
                send_attention()

    with scope('atwait'):
        all_bytes(arecv, group - 1, at_s, at_r).wait_recv()

    with scope('final'):
        attn = arecv[...].astype(F32).reshape(batch, q_cols).astype(BF16)
        total = (acc[...] + jnp.dot(attn, wo[0:q_cols, :], preferred_element_type=F32)).astype(BF16)
        for cc in range(cols):
            total_ref[cc] = total[:, cc * xw:(cc + 1) * xw]
        for j in range(cols):
            y_refs[j][...] = total_ref[(c + j) % cols]

    all_bytes(st, group - 1, st_s, st_r).wait_send()
    all_bytes(qsend, group - 1, q_s, q_r).wait_send()
    all_bytes(arecv, group - 1, at_s, at_r).wait_send()
    all_bytes(xg, cols - 1, xs_s, xs_r).wait_send()
    all_bytes(gg, cols - 1, g_s, g_r).wait_send()
    for d in range(2):
        @pl.when(pos[d] < rows - 1)
        def _():
            all_bytes(part.at[d], n_chunks, rs_s.at[d], rs_s.at[d]).wait_send()

        @pl.when(pos[d] > 0)
        def _():
            all_bytes(mful.at[d], n_chunks, ag_s.at[d], ag_s.at[d]).wait_send()


def store_kernel(kbuf, vbuf, k_out, v_out, sem):
    copies = [pltpu.make_async_copy(src.at[b], dst.at[b], sem.at[i, b])
              for b in range(kbuf.shape[0]) for i, (src, dst) in enumerate(((kbuf, k_out), (vbuf, v_out)))]
    for copy in copies:
        copy.start()
    for copy in copies:
        copy.wait()


def solution(mesh):
    rows = mesh.shape['row']
    cols = mesh.shape['col']
    seq_spec = P(('dp', 'col', 'row'))
    act_spec = P('dp', ('row', 'col'))

    def local_layer(x, ln_gain, w_in, w_out, k_cache, v_cache, lengths, rope_cos, rope_sin):
        batch, xw = x.shape
        group = rows * cols
        seqs = batch // group
        head = rope_cos.shape[1] * 2
        cache_len = k_cache.shape[1]
        kdim, e_cols = w_in.shape
        r_cols, n_out = w_out.shape
        kv_cols = head // cols
        f_cols = e_cols - r_cols - 2 * kv_cols
        q_cols = r_cols - f_cols
        gate_start = q_cols + 2 * kv_cols
        heads = q_cols * cols // head
        w = CHUNK
        n_chunks = f_cols // 2 // w
        dims = (rows, cols, n_chunks, w, q_cols, kv_cols, f_cols)
        vmem = pl.BlockSpec(memory_space=pltpu.VMEM)
        hbm = pl.BlockSpec(memory_space=pl.ANY)
        dma = pltpu.SemaphoreType.DMA
        pieces, k_all, v_all = pl.pallas_call(
            functools.partial(layer_kernel, dims),
            out_shape=((jax.ShapeDtypeStruct((batch, xw), BF16),) * cols, pltpu.VMEM((seqs, cache_len, head), BF16),
                       pltpu.VMEM((seqs, cache_len, head), BF16)),
            in_specs=[hbm] * 9,
            out_specs=((vmem,) * cols, vmem, vmem),
            scratch_shapes=[
                pltpu.SMEM((seqs,), jnp.int32),
                pltpu.VMEM((xw,), BF16),
                pltpu.VMEM((seqs, head // 2), F32),
                pltpu.VMEM((seqs, head // 2), F32),
                pltpu.VMEM((kdim, gate_start), BF16),
                pltpu.VMEM((n_chunks, kdim, 4 * w), BF16),
                pltpu.VMEM((r_cols, n_out), BF16),
                pltpu.VMEM((cols, batch, xw), BF16),
                pltpu.VMEM((cols, 8, xw), F32),
                pltpu.VMEM((group, 8, batch), F32),
                pltpu.VMEM((batch, kdim), BF16),
                pltpu.VMEM((2, n_chunks, batch, 2 * w), BF16),
                pltpu.VMEM((2, n_chunks, batch, 2 * w), BF16),
                pltpu.VMEM((2, n_chunks, batch, w), BF16),
                pltpu.VMEM((group, seqs, gate_start), BF16),
                pltpu.VMEM((group, seqs, gate_start), BF16),
                pltpu.VMEM((heads, seqs, head), F32),
                pltpu.VMEM((seqs, heads, head), BF16),
                pltpu.VMEM((seqs, 8, head), F32),
                pltpu.VMEM((seqs, 8, head), F32),
                pltpu.VMEM((seqs, heads, head), F32),
                pltpu.VMEM((cols, seqs, q_cols), BF16),
                pltpu.VMEM((group, seqs, q_cols), BF16),
                pltpu.VMEM((batch, n_out), F32),
                pltpu.VMEM((cols, batch, xw), BF16),
                dma((5,)), dma((n_chunks + 2,)), dma((seqs,)),
                dma(()), dma(()), dma(()), dma(()), dma(()), dma(()), dma(()), dma(()),
                dma((2,)), dma((2, n_chunks)), dma((2,)), dma((2, n_chunks)),
                dma(()), dma(()),
            ],
            compiler_params=pltpu.CompilerParams(collective_id=0, has_side_effects=True,
                                                 vmem_limit_bytes=44 * 1024 * 1024),
            name="layer",
        )(lengths, x, ln_gain, w_in, w_out, k_cache, v_cache, rope_cos, rope_sin)
        delta = pieces[0].astype(F32)
        for j in range(1, cols):
            moved = lax.ppermute(pieces[j], 'col', [(s, (s + j) % cols) for s in range(cols)])
            delta = delta + moved.astype(F32)
        cache_bytes = 2 * k_all.size * 2
        k_out, v_out = pl.pallas_call(
            store_kernel,
            out_shape=(jax.ShapeDtypeStruct(k_all.shape, BF16),) * 2,
            in_specs=[vmem, vmem],
            out_specs=(hbm, hbm),
            scratch_shapes=[dma((2, seqs))],
            cost_estimate=pl.CostEstimate(flops=10 ** 8, bytes_accessed=cache_bytes, transcendentals=0),
            compiler_params=pltpu.CompilerParams(vmem_limit_bytes=1024 * 1024),
            name="store",
        )(k_all, v_all)
        y = (x.astype(F32) + delta.astype(BF16).astype(F32)).astype(BF16)
        return y, k_out, v_out

    return jax.shard_map(local_layer, mesh=mesh, in_specs=(act_spec, P(('row', 'col')), P('row', 'col'), P('col', 'row'), seq_spec, seq_spec, seq_spec, seq_spec, seq_spec), out_specs=(act_spec, seq_spec, seq_spec), check_vma=False)
```

time: 86 us -> 76.8 us (0.89)
  local copies, waits for them, and re-layouts: 8.65 us -> 0.01 us
  Pallas kernels: 76.6 us -> 72.5 us
  starting transfers between devices: 0 us -> 2.75 us
    unnamed x5 -> x4, local copies, waits for them, and re-layouts: 7.43 us -> 0.01 us
    pallas_call x1 -> x2, Pallas kernels: 76.6 us -> 72.5 us  [the longest x1 66.6 us: local_layer(): pl.pallas_call(functools.partial(layer_kernel, dims), out_shape=((jax.Sha...]
    ppermute x0 -> x3, starting transfers between devices: none -> 2.75 us  [local_layer(): lax.ppermute(pieces[j], 'col', [(s, (s + j) % cols) for s in range(cols)])]
    broadcast_in_dim x1 -> x0, local copies, waits for them, and re-layouts: 1.22 us -> none  [local_layer(): ln_gain[None, :]]
  transfers between devices with their start and end apart: 0 -> 3, of which waited for: 0 -> 0; matrix products, arithmetic and copies ran while one was open for 0% -> 0% of each run, Pallas kernels for 0% -> 8%
where the time goes in v3:
time: 76.8 us; the launch traced here: 76.7 us
  Pallas kernels  72.5 us (94%)
  starting transfers between devices  2.75 us (4%)
    pallas_call x1, Pallas kernels, local_layer(): pl.pallas_call(functools.partial(layer_kernel, dims), out_shape=((jax.Sha...  66.6 us
    pallas_call x1, Pallas kernels, local_layer(): pl.pallas_call(store_kernel, out_shape=(jax.ShapeDtypeStruct(k_all.shape,...  5.96 us
    ppermute x3, starting transfers between devices, local_layer(): lax.ppermute(pieces[j], 'col', [(s, (s + j) % cols) for s in range(cols)])  2.75 us
  transfers between devices with their start and end apart: 3, of which 0 were waited for; matrix products, arithmetic and copies ran while one was open for 0% of the time, Pallas kernels for 8%

profile of v3, /device:TPU:0, one launch (start us, length us, event | category | flops | bytes accessed | tf_op | source)
XLA Modules:
  0.0 76.7 jit_solution(9564344986165961939)
XLA Ops:
  0.6 66.6 %layer.1 = (bf16[128,256]{1,0:T(8,128)(2,1)}, bf16[128,256]{1,0:T(8,128)(2,1)}, bf16[128,256]{1,0:T(8,128)(2,1)}, bf16[128,256]{1,0:T(8,128)(2,1)}, bf16[8,2048,...) custom-call(s32[8]{0:T(128)} %len_hbm.1, bf16[128,256]{1,0:T(8,128)(2,1)} %x_hbm.1, bf16[256]{0:T(256)(128)(2,1)} %gain_hbm.1, ...), custom_call_target="tpu_custom_call" | custom-call | tf_op jit(solution)/shard_map/layer/pallas_call | solution.py:396
  67.2 0.1 collective-permute-start
  67.3 1.3 %collective-permute-start.1 = (bf16[128,256]{1,0:T(8,128)(2,1)}, bf16[128,256]{1,0:T(8,128)(2,1)S(1)}, u32[]{:S(2)}, u32[]{:S(2)}) collective-permute-start(bf16[128,256]{1,0:T(8,128)(2,1)} %get-tuple-element.13), channel_id=1, source_target_pairs={{0,2},{1,3},{2,0},{3,1},{4,6},{5,7},{6,4},{7,5},{8,10},{9,11},{10,... | collective-permute-start | bytes 196616 | tf_op jit(solution)/shard_map/ppermute | solution.py:439
  68.6 1.4 %collective-permute-start.2 = (bf16[128,256]{1,0:T(8,128)(2,1)}, bf16[128,256]{1,0:T(8,128)(2,1)S(1)}, u32[]{:S(2)}, u32[]{:S(2)}) collective-permute-start(bf16[128,256]{1,0:T(8,128)(2,1)} %get-tuple-element.14), channel_id=1, source_target_pairs={{0,3},{1,0},{2,1},{3,2},{4,7},{5,4},{6,5},{7,6},{8,11},{9,8},{10,9... | collective-permute-start | bytes 196616 | tf_op jit(solution)/shard_map/ppermute | solution.py:439
  70.0 0.0 copy-start
  70.0 0.0 copy-start.1
  70.0 6.0 %store.1 = (bf16[8,2048,256]{2,1,0:T(8,128)(2,1)}, bf16[8,2048,256]{2,1,0:T(8,128)(2,1)}) custom-call(bf16[8,2048,256]{2,1,0:T(8,128)(2,1)S(1)} %get-tuple-element.15.kbuf, bf16[8,2048,256]{2,1,0:T(8,128)(2,1)S(1)} %get-tuple-element.16.vbuf), custom_call_target="tpu_custom_call" | custom-call | flops 100000000 | bytes 16777216 | tf_op jit(solution)/shard_map/store/pallas_call | solution.py:442
  75.9 0.0 collective-permute-done
  75.9 0.0 collective-permute-done.1
  76.0 0.0 collective-permute-done.2
  76.0 0.0 copy-done
  76.0 0.0 copy-done.1
  76.0 0.7 add_convert_fusion
Async XLA Ops:
  67.2 8.7 %collective-permute-start = (bf16[128,256]{1,0:T(8,128)(2,1)}, bf16[128,256]{1,0:T(8,128)(2,1)S(1)}, u32[]{:S(2)}, u32[]{:S(2)}) collective-permute-start(bf16[128,256]{1,0:T(8,128)(2,1)} %get-tuple-element.12), channel_id=1, source_target_pairs={{0,1},{1,2},{2,3},{3,0},{4,5},{5,6},{6,7},{7,4},{8,9},{9,10},{10,1... | collective-permute-start | bytes 196616 | tf_op jit(solution)/shard_map/ppermute | solution.py:439
  67.3 8.7 %collective-permute-start.1 = (bf16[128,256]{1,0:T(8,128)(2,1)}, bf16[128,256]{1,0:T(8,128)(2,1)S(1)}, u32[]{:S(2)}, u32[]{:S(2)}) collective-permute-start(bf16[128,256]{1,0:T(8,128)(2,1)} %get-tuple-element.13), channel_id=1, source_target_pairs={{0,2},{1,3},{2,0},{3,1},{4,6},{5,7},{6,4},{7,5},{8,10},{9,11},{10,... | collective-permute-start | bytes 196616 | tf_op jit(solution)/shard_map/ppermute | solution.py:439
  68.6 7.4 %collective-permute-start.2 = (bf16[128,256]{1,0:T(8,128)(2,1)}, bf16[128,256]{1,0:T(8,128)(2,1)S(1)}, u32[]{:S(2)}, u32[]{:S(2)}) collective-permute-start(bf16[128,256]{1,0:T(8,128)(2,1)} %get-tuple-element.14), channel_id=1, source_target_pairs={{0,3},{1,0},{2,1},{3,2},{4,7},{5,4},{6,5},{7,6},{8,11},{9,8},{10,9... | collective-permute-start | bytes 196616 | tf_op jit(solution)/shard_map/ppermute | solution.py:439
  70.0 6.0 %copy-start = (bf16[128,256]{1,0:T(8,128)(2,1)S(1)}, bf16[128,256]{1,0:T(8,128)(2,1)}, u32[]{:S(2)}) copy-start(bf16[128,256]{1,0:T(8,128)(2,1)} %x_hbm.1) | copy-start | bytes 196612
  70.0 6.0 %copy-start.1 = (bf16[128,256]{1,0:T(8,128)(2,1)S(1)}, bf16[128,256]{1,0:T(8,128)(2,1)}, u32[]{:S(2)}) copy-start(bf16[128,256]{1,0:T(8,128)(2,1)} %get-tuple-element.11) | copy-start | bytes 196612

commit v4 on v3

--- a/solution.py
+++ b/solution.py
@@ -17,9 +17,10 @@
 BEFORE = 8
 LAG = 3
 ATTN_AT = 7
-SEND_AT = 18
+SEND_AT = 15
+SPREAD = 3
 GATHER_AT = 15
-GATHER_LAG = 3
+GATHER_LAG = 2
 PROFILE = False
 
 
@@ -28,15 +29,15 @@
 
 
 def layer_kernel(dims, len_hbm, x_hbm, gain_hbm, win_ref, wout_ref, kc_ref, vc_ref, cos_hbm, sin_hbm,
-                 y_refs, kbuf, vbuf,
+                 mine_ref, other_ref, kbuf, vbuf,
                  len_ref, gain_ref, cos_ref, sin_ref, wq, wgu, wo, xg, gg, st, h, part, rbuf, mful, qsend, qrecv, qhm, qsm, kn3, vn3, osm,
-                 asend, arecv, acc, total_ref,
-                 isem, wsem, kvsem, xs_s, xs_r, g_s, g_r, st_s, st_r, q_s, q_r, rs_s, rs_r, ag_s, ag_r, at_s, at_r):
+                 asend, arecv, acc, total_ref, pair,
+                 isem, wsem, kvsem, xs_s, xs_r, g_s, g_r, st_s, st_r, q_s, q_r, rs_s, rs_r, ag_s, ag_r, ac_s, ac_r, ab_s, ab_r, pr_s, pr_r):
     rows, cols, n_chunks, w, q_cols, kv_cols, f_cols = dims
     group = rows * cols
     dp, r, c = lax.axis_index("dp"), lax.axis_index("row"), lax.axis_index("col")
     me = c * rows + r
-    batch, xw = y_refs[0].shape
+    batch, xw = mine_ref.shape
     seqs = batch // group
     gate_start = q_cols + 2 * kv_cols
     half_f = f_cols // 2
@@ -239,18 +240,37 @@
         probs = (e / jnp.sum(e, axis=1, keepdims=True)).astype(BF16)
         osm[b] = jnp.dot(probs, v_all, preferred_element_type=F32)
 
-    def at_copy(slot, peer):
-        return pltpu.make_async_remote_copy(asend.at[peer // rows], arecv.at[slot], at_s, at_r,
-                                            device_id=dev(peer), device_id_type=MESH)
+    def ac_copy(peer_c):
+        return pltpu.make_async_remote_copy(asend.at[peer_c], arecv.at[r, c], ac_s, ac_r,
+                                            device_id=(dp, r, peer_c), device_id_type=MESH)
+
+    def ab_copy(d, rr):
+        return pltpu.make_async_remote_copy(arecv.at[rr], arecv.at[rr], ab_s.at[d, rr], ab_r.at[d, rr],
+                                            device_id=(dp, r + 1 - 2 * d, c), device_id_type=MESH)
 
     def send_attention():
         for cc in range(cols):
             asend[cc] = jnp.concatenate([osm[:, cc * heads_c + i, :] for i in range(heads_c)], axis=-1).astype(BF16)
-        arecv[me] = asend[c]
-
-        @pl.loop(1, group)
+        arecv[r, c] = asend[c]
+
+        @pl.loop(1, cols)
         def _(j):
-            at_copy(me, (me + j) % group).start()
+            ac_copy((c + j) % cols).start()
+
+    def spread_attention(t):
+        if t == 0:
+            all_bytes(arecv.at[r], cols - 1, ac_s, ac_r).wait_recv()
+        for d in range(2):
+            rr = r - t + 2 * t * d
+
+            @pl.when(t <= pos[d])
+            def _():
+                if t > 0:
+                    ab_copy(d, rr).wait_recv()
+
+                @pl.when(pos[d] < rows - 1)
+                def _():
+                    ab_copy(d, rr).start()
 
     @pl.loop(0, FIRST)
     def _(k):
@@ -276,7 +296,7 @@
         with scope('partial'):
             partial_step(k)
 
-    @pl.loop(0, max(GATHER_AT + GATHER_LAG * (rows - 2) + n_chunks // 2, LAG * (rows - 2) + n_chunks))
+    @pl.loop(0, max(GATHER_AT + GATHER_LAG * (rows - 2) + n_chunks // 2, SEND_AT + SPREAD * rows + 1, LAG * (rows - 2) + n_chunks))
     def _(i):
         @pl.when(i == LAG)
         def _():
@@ -333,20 +353,31 @@
             with scope('sendattn'):
                 send_attention()
 
-    with scope('atwait'):
-        all_bytes(arecv, group - 1, at_s, at_r).wait_recv()
+        for t in range(rows):
+            @pl.when(i == SEND_AT + SPREAD * (t + 1))
+            def _():
+                with scope('spread%d' % t):
+                    spread_attention(t)
 
     with scope('final'):
-        attn = arecv[...].astype(F32).reshape(batch, q_cols).astype(BF16)
+        attn = jnp.concatenate([arecv[rr, cc].astype(F32) for cc in range(cols) for rr in range(rows)], axis=0).astype(BF16)
         total = (acc[...] + jnp.dot(attn, wo[0:q_cols, :], preferred_element_type=F32)).astype(BF16)
         for cc in range(cols):
             total_ref[cc] = total[:, cc * xw:(cc + 1) * xw]
-        for j in range(cols):
-            y_refs[j][...] = total_ref[(c + j) % cols]
+
+    mate = c + 1 - 2 * (c % 2)
+    across = (c + 2) % cols
+
+    def pair_copy(i):
+        return pltpu.make_async_remote_copy(total_ref.at[(mate + 2 * i) % cols], pair.at[i], pr_s, pr_r,
+                                            device_id=(dp, r, mate), device_id_type=MESH)
+
+    pair_copy(1).start()
+    pair_copy(0).start()
 
     all_bytes(st, group - 1, st_s, st_r).wait_send()
     all_bytes(qsend, group - 1, q_s, q_r).wait_send()
-    all_bytes(arecv, group - 1, at_s, at_r).wait_send()
+    all_bytes(asend, cols - 1, ac_s, ac_r).wait_send()
     all_bytes(xg, cols - 1, xs_s, xs_r).wait_send()
     all_bytes(gg, cols - 1, g_s, g_r).wait_send()
     for d in range(2):
@@ -354,9 +385,20 @@
         def _():
             all_bytes(part.at[d], n_chunks, rs_s.at[d], rs_s.at[d]).wait_send()
 
+            for t in range(rows):
+                @pl.when(t <= pos[d])
+                def _():
+                    ab_copy(d, r - t + 2 * t * d).wait_send()
+
         @pl.when(pos[d] > 0)
         def _():
             all_bytes(mful.at[d], n_chunks, ag_s.at[d], ag_s.at[d]).wait_send()
+
+    with scope('pair'):
+        all_bytes(pair, 2, pr_s, pr_r).wait_recv()
+    other_ref[...] = (total_ref[across].astype(F32) + pair[1].astype(F32)).astype(BF16)
+    mine_ref[...] = total_ref[c].astype(F32) + pair[0].astype(F32)
+    all_bytes(pair, 2, pr_s, pr_r).wait_send()
 
 
 def store_kernel(kbuf, vbuf, k_out, v_out, sem):
@@ -393,12 +435,12 @@
         vmem = pl.BlockSpec(memory_space=pltpu.VMEM)
         hbm = pl.BlockSpec(memory_space=pl.ANY)
         dma = pltpu.SemaphoreType.DMA
-        pieces, k_all, v_all = pl.pallas_call(
+        mine, other, k_all, v_all = pl.pallas_call(
             functools.partial(layer_kernel, dims),
-            out_shape=((jax.ShapeDtypeStruct((batch, xw), BF16),) * cols, pltpu.VMEM((seqs, cache_len, head), BF16),
+            out_shape=(pltpu.VMEM((batch, xw), F32), pltpu.VMEM((batch, xw), BF16), pltpu.VMEM((seqs, cache_len, head), BF16),
                        pltpu.VMEM((seqs, cache_len, head), BF16)),
             in_specs=[hbm] * 9,
-            out_specs=((vmem,) * cols, vmem, vmem),
+            out_specs=(vmem, vmem, vmem, vmem),
             scratch_shapes=[
                 pltpu.SMEM((seqs,), jnp.int32),
                 pltpu.VMEM((xw,), BF16),
@@ -422,22 +464,21 @@
                 pltpu.VMEM((seqs, 8, head), F32),
                 pltpu.VMEM((seqs, heads, head), F32),
                 pltpu.VMEM((cols, seqs, q_cols), BF16),
-                pltpu.VMEM((group, seqs, q_cols), BF16),
+                pltpu.VMEM((rows, cols, seqs, q_cols), BF16),
                 pltpu.VMEM((batch, n_out), F32),
                 pltpu.VMEM((cols, batch, xw), BF16),
+                pltpu.VMEM((2, batch, xw), BF16),
                 dma((5,)), dma((n_chunks + 2,)), dma((seqs,)),
                 dma(()), dma(()), dma(()), dma(()), dma(()), dma(()), dma(()), dma(()),
                 dma((2,)), dma((2, n_chunks)), dma((2,)), dma((2, n_chunks)),
-                dma(()), dma(()),
+                dma(()), dma(()), dma((2, rows)), dma((2, rows)), dma(()), dma(()),
             ],
             compiler_params=pltpu.CompilerParams(collective_id=0, has_side_effects=True,
                                                  vmem_limit_bytes=44 * 1024 * 1024),
             name="layer",
         )(lengths, x, ln_gain, w_in, w_out, k_cache, v_cache, rope_cos, rope_sin)
-        delta = pieces[0].astype(F32)
-        for j in range(1, cols):
-            moved = lax.ppermute(pieces[j], 'col', [(s, (s + j) % cols) for s in range(cols)])
-            delta = delta + moved.astype(F32)
+        moved = lax.ppermute(other, 'col', [(s, (s + 2) % cols) for s in range(cols)])
+        delta = mine + moved.astype(F32)
         cache_bytes = 2 * k_all.size * 2
         k_out, v_out = pl.pallas_call(
             store_kernel,

time: 76.8 us -> 75.7 us (0.986)
  starting transfers between devices: 2.75 us -> 1.17 us
    ppermute x3 -> x1, starting transfers between devices: 2.75 us -> 1.17 us  [local_layer(): lax.ppermute(other, 'col', [(s, (s + 2) % cols) for s in range(cols)])]
  transfers between devices with their start and end apart: 3 -> 1, of which waited for: 0 -> 0; matrix products, arithmetic and copies ran while one was open for 0% -> 0% of each run, Pallas kernels for 8% -> 8%
where the time goes in v4:
time: 75.7 us; the launch traced here: 75.6 us
  Pallas kernels  73.1 us (97%)
  starting transfers between devices  1.17 us (2%)
    pallas_call x1, Pallas kernels, local_layer(): pl.pallas_call(functools.partial(layer_kernel, dims), out_shape=(pltpu.VM...  67.1 us
    pallas_call x1, Pallas kernels, local_layer(): pl.pallas_call(store_kernel, out_shape=(jax.ShapeDtypeStruct(k_all.shape,...  5.96 us
  transfers between devices with their start and end apart: 1, of which 0 were waited for; matrix products, arithmetic and copies ran while one was open for 0% of the time, Pallas kernels for 8%

profile of v4, /device:TPU:0, one launch (start us, length us, event | category | flops | bytes accessed | tf_op | source)
XLA Modules:
  0.0 75.6 jit_solution(5573056670674322159)
XLA Ops:
  0.6 67.1 %layer.1 = (f32[128,256]{1,0:T(8,128)S(1)}, bf16[128,256]{1,0:T(8,128)(2,1)S(1)}, bf16[8,2048,256]{2,1,0:T(8,128)(2,1)S(1)}, bf16[8,2048,256]{2,1,0:T(8,128)(2,1)S(1)}) custom-call(s32[8]{0:T(128)} %len_hbm.1, bf16[128,256]{1,0:T(8,128)(2,1)} %x_hbm.1, bf16[256]{0:T(256)(128)(2,1)} %gain_hbm.1, bf16[1024,9344]{1,0:T(8,128)(2,1)} %win_ref.1, ...), custom_call_target="tpu_custom_call" | custom-call | tf_op jit(solution)/shard_map/layer/pallas_call | solution.py:438
  67.7 1.2 %collective-permute-start = (bf16[128,256]{1,0:T(8,128)(2,1)S(1)}, bf16[128,256]{1,0:T(8,128)(2,1)S(1)}, u32[]{:S(2)}, u32[]{:S(2)}) collective-permute-start(bf16[128,256]{1,0:T(8,128)(2,1)S(1)} %get-tuple-element.10), channel_id=1, source_target_pairs={{0,2},{1,3},{2,0},{3,1},{4,6},{5,7},{6,4},{7,5},{8,10},{9,11},{10,... | collective-permute-start | bytes 196616 | tf_op jit(solution)/shard_map/ppermute | solution.py:480
  68.9 0.0 copy-start
  68.9 6.0 %store.1 = (bf16[8,2048,256]{2,1,0:T(8,128)(2,1)}, bf16[8,2048,256]{2,1,0:T(8,128)(2,1)}) custom-call(bf16[8,2048,256]{2,1,0:T(8,128)(2,1)S(1)} %get-tuple-element.11.kbuf, bf16[8,2048,256]{2,1,0:T(8,128)(2,1)S(1)} %get-tuple-element.12.vbuf), custom_call_target="tpu_custom_call" | custom-call | flops 100000000 | bytes 16777216 | tf_op jit(solution)/shard_map/store/pallas_call | solution.py:483
  74.9 0.0 collective-permute-done
  74.9 0.0 copy-done
  74.9 0.7 add_convert_fusion
Async XLA Ops:
  67.7 7.1 %collective-permute-start = (bf16[128,256]{1,0:T(8,128)(2,1)S(1)}, bf16[128,256]{1,0:T(8,128)(2,1)S(1)}, u32[]{:S(2)}, u32[]{:S(2)}) collective-permute-start(bf16[128,256]{1,0:T(8,128)(2,1)S(1)} %get-tuple-element.10), channel_id=1, source_target_pairs={{0,2},{1,3},{2,0},{3,1},{4,6},{5,7},{6,4},{7,5},{8,10},{9,11},{10,... | collective-permute-start | bytes 196616 | tf_op jit(solution)/shard_map/ppermute | solution.py:480
  68.9 6.0 %copy-start = (bf16[128,256]{1,0:T(8,128)(2,1)S(1)}, bf16[128,256]{1,0:T(8,128)(2,1)}, u32[]{:S(2)}) copy-start(bf16[128,256]{1,0:T(8,128)(2,1)} %x_hbm.1) | copy-start | bytes 196612

commit v5 on v4

--- a/solution.py
+++ b/solution.py
@@ -15,10 +15,10 @@
 CHUNK = 128
 FIRST = 4
 BEFORE = 8
-LAG = 3
+LAG = 2
 ATTN_AT = 7
 SEND_AT = 15
-SPREAD = 3
+SPREAD = 2
 GATHER_AT = 15
 GATHER_LAG = 2
 PROFILE = False
@@ -309,10 +309,23 @@
                     partial_step(BEFORE + 2 * i + half)
 
         for d in range(2):
+            @pl.when((pos[d] == 1) & (i < n_chunks))
+            def _():
+                with scope('rswait%d' % d):
+                    rs_copy(d, i).wait_recv()
+                part[d, i] = (part[d, i].astype(F32) + rbuf[d, i].astype(F32)).astype(BF16)
+                rs_copy(d, i).start()
+
+        @pl.when((i >= ATTN_AT) & (i < ATTN_AT + seqs))
+        def _():
+            with scope('attend'):
+                attend(i - ATTN_AT)
+
+        for d in range(2):
             p = pos[d]
             k = i - LAG * (p - 1)
 
-            @pl.when((p > 0) & (k >= 0) & (k < n_chunks))
+            @pl.when((p > 1) & (k >= 0) & (k < n_chunks))
             def _():
                 with scope('rswait%d' % d):
                     rs_copy(d, k).wait_recv()
@@ -343,11 +356,6 @@
                     copy.wait()
                 prepare_queries()
 
-        @pl.when((i >= ATTN_AT) & (i < ATTN_AT + seqs))
-        def _():
-            with scope('attend'):
-                attend(i - ATTN_AT)
-
         @pl.when(i == SEND_AT)
         def _():
             with scope('sendattn'):
@@ -358,10 +366,12 @@
             def _():
                 with scope('spread%d' % t):
                     spread_attention(t)
+                    if t == rows - 1:
+                        attn = jnp.concatenate([arecv[rr, cc].astype(F32) for cc in range(cols) for rr in range(rows)], axis=0)
+                        acc[...] += jnp.dot(attn.astype(BF16), wo[0:q_cols, :], preferred_element_type=F32)
 
     with scope('final'):
-        attn = jnp.concatenate([arecv[rr, cc].astype(F32) for cc in range(cols) for rr in range(rows)], axis=0).astype(BF16)
-        total = (acc[...] + jnp.dot(attn, wo[0:q_cols, :], preferred_element_type=F32)).astype(BF16)
+        total = acc[...].astype(BF16)
         for cc in range(cols):
             total_ref[cc] = total[:, cc * xw:(cc + 1) * xw]
 

time: 75.7 us -> 75 us (level)
  no operation moved by 1% of the time
where the time goes in v5:
time: 75 us; the launch traced here: 74.8 us
  Pallas kernels  72.5 us (97%)
  starting transfers between devices  1.02 us (1%)
    pallas_call x1, Pallas kernels, local_layer(): pl.pallas_call(functools.partial(layer_kernel, dims), out_shape=(pltpu.VM...  66.5 us
    pallas_call x1, Pallas kernels, local_layer(): pl.pallas_call(store_kernel, out_shape=(jax.ShapeDtypeStruct(k_all.shape,...  5.96 us
  transfers between devices with their start and end apart: 1, of which 0 were waited for; matrix products, arithmetic and copies ran while one was open for 0% of the time, Pallas kernels for 8%

profile of v5, /device:TPU:0, one launch (start us, length us, event | category | flops | bytes accessed | tf_op | source)
XLA Modules:
  0.0 74.8 jit_solution(15305698693774309339)
XLA Ops:
  0.6 66.5 %layer.1 = (f32[128,256]{1,0:T(8,128)S(1)}, bf16[128,256]{1,0:T(8,128)(2,1)S(1)}, bf16[8,2048,256]{2,1,0:T(8,128)(2,1)S(1)}, bf16[8,2048,256]{2,1,0:T(8,128)(2,1)S(1)}) custom-call(s32[8]{0:T(128)} %len_hbm.1, bf16[128,256]{1,0:T(8,128)(2,1)} %x_hbm.1, bf16[256]{0:T(256)(128)(2,1)} %gain_hbm.1, bf16[1024,9344]{1,0:T(8,128)(2,1)} %win_ref.1, ...), custom_call_target="tpu_custom_call" | custom-call | tf_op jit(solution)/shard_map/layer/pallas_call | solution.py:448
  67.2 1.0 %collective-permute-start = (bf16[128,256]{1,0:T(8,128)(2,1)S(1)}, bf16[128,256]{1,0:T(8,128)(2,1)S(1)}, u32[]{:S(2)}, u32[]{:S(2)}) collective-permute-start(bf16[128,256]{1,0:T(8,128)(2,1)S(1)} %get-tuple-element.10), channel_id=1, source_target_pairs={{0,2},{1,3},{2,0},{3,1},{4,6},{5,7},{6,4},{7,5},{8,10},{9,11},{10,... | collective-permute-start | bytes 196616 | tf_op jit(solution)/shard_map/ppermute | solution.py:490
  68.2 0.0 copy-start
  68.2 6.0 %store.1 = (bf16[8,2048,256]{2,1,0:T(8,128)(2,1)}, bf16[8,2048,256]{2,1,0:T(8,128)(2,1)}) custom-call(bf16[8,2048,256]{2,1,0:T(8,128)(2,1)S(1)} %get-tuple-element.11.kbuf, bf16[8,2048,256]{2,1,0:T(8,128)(2,1)S(1)} %get-tuple-element.12.vbuf), custom_call_target="tpu_custom_call" | custom-call | flops 100000000 | bytes 16777216 | tf_op jit(solution)/shard_map/store/pallas_call | solution.py:493
  74.1 0.0 collective-permute-done
  74.1 0.0 copy-done
  74.2 0.7 add_convert_fusion
Async XLA Ops:
  67.2 7.0 %collective-permute-start = (bf16[128,256]{1,0:T(8,128)(2,1)S(1)}, bf16[128,256]{1,0:T(8,128)(2,1)S(1)}, u32[]{:S(2)}, u32[]{:S(2)}) collective-permute-start(bf16[128,256]{1,0:T(8,128)(2,1)S(1)} %get-tuple-element.10), channel_id=1, source_target_pairs={{0,2},{1,3},{2,0},{3,1},{4,6},{5,7},{6,4},{7,5},{8,10},{9,11},{10,... | collective-permute-start | bytes 196616 | tf_op jit(solution)/shard_map/ppermute | solution.py:490
  68.2 6.0 %copy-start = (bf16[128,256]{1,0:T(8,128)(2,1)S(1)}, bf16[128,256]{1,0:T(8,128)(2,1)}, u32[]{:S(2)}) copy-start(bf16[128,256]{1,0:T(8,128)(2,1)} %x_hbm.1) | copy-start | bytes 196612

commit v6 on v5

--- a/solution.py
+++ b/solution.py
@@ -120,14 +120,14 @@
         return pltpu.make_async_remote_copy(gg.at[slot], gg.at[slot], g_s, g_r,
                                             device_id=(dp, r, peer_c), device_id_type=MESH)
 
+    @pl.loop(1, cols)
+    def _(j):
+        g_copy(c, (c + j) % cols).start()
+        x_copy(c, (c + j) % cols).start()
+
     @pl.loop(1, group)
     def _(j):
         st_copy(me, (me + j) % group).start()
-
-    @pl.loop(1, cols)
-    def _(j):
-        x_copy(c, (c + j) % cols).start()
-        g_copy(c, (c + j) % cols).start()
 
 
     with scope('stats'):

time: 75 us -> 75.7 us (level)
  no operation moved by 1% of the time
where the time goes in v6:
time: 75.7 us; the launch traced here: 75.6 us
  Pallas kernels  72.7 us (96%)
  starting transfers between devices  1.6 us (2%)
    pallas_call x1, Pallas kernels, local_layer(): pl.pallas_call(functools.partial(layer_kernel, dims), out_shape=(pltpu.VM...  66.7 us
    pallas_call x1, Pallas kernels, local_layer(): pl.pallas_call(store_kernel, out_shape=(jax.ShapeDtypeStruct(k_all.shape,...  5.96 us
    ppermute x1, starting transfers between devices, local_layer(): lax.ppermute(other, 'col', [(s, (s + 2) % cols) for s in range(cols)])  1.6 us
  transfers between devices with their start and end apart: 1, of which 0 were waited for; matrix products, arithmetic and copies ran while one was open for 0% of the time, Pallas kernels for 8%

profile of v6, /device:TPU:0, one launch (start us, length us, event | category | flops | bytes accessed | tf_op | source)
XLA Modules:
  0.0 75.6 jit_solution(12124052333719073844)
XLA Ops:
  0.6 66.7 %layer.1 = (f32[128,256]{1,0:T(8,128)S(1)}, bf16[128,256]{1,0:T(8,128)(2,1)S(1)}, bf16[8,2048,256]{2,1,0:T(8,128)(2,1)S(1)}, bf16[8,2048,256]{2,1,0:T(8,128)(2,1)S(1)}) custom-call(s32[8]{0:T(128)} %len_hbm.1, bf16[128,256]{1,0:T(8,128)(2,1)} %x_hbm.1, bf16[256]{0:T(256)(128)(2,1)} %gain_hbm.1, bf16[1024,9344]{1,0:T(8,128)(2,1)} %win_ref.1, ...), custom_call_target="tpu_custom_call" | custom-call | tf_op jit(solution)/shard_map/layer/pallas_call | solution.py:448
  67.3 1.6 %collective-permute-start = (bf16[128,256]{1,0:T(8,128)(2,1)S(1)}, bf16[128,256]{1,0:T(8,128)(2,1)S(1)}, u32[]{:S(2)}, u32[]{:S(2)}) collective-permute-start(bf16[128,256]{1,0:T(8,128)(2,1)S(1)} %get-tuple-element.10), channel_id=1, source_target_pairs={{0,2},{1,3},{2,0},{3,1},{4,6},{5,7},{6,4},{7,5},{8,10},{9,11},{10,... | collective-permute-start | bytes 196616 | tf_op jit(solution)/shard_map/ppermute | solution.py:490
  68.9 0.0 copy-start
  68.9 6.0 %store.1 = (bf16[8,2048,256]{2,1,0:T(8,128)(2,1)}, bf16[8,2048,256]{2,1,0:T(8,128)(2,1)}) custom-call(bf16[8,2048,256]{2,1,0:T(8,128)(2,1)S(1)} %get-tuple-element.11.kbuf, bf16[8,2048,256]{2,1,0:T(8,128)(2,1)S(1)} %get-tuple-element.12.vbuf), custom_call_target="tpu_custom_call" | custom-call | flops 100000000 | bytes 16777216 | tf_op jit(solution)/shard_map/store/pallas_call | solution.py:493
  74.9 0.0 collective-permute-done
  74.9 0.0 copy-done
  74.9 0.7 add_convert_fusion
Async XLA Ops:
  67.3 7.6 %collective-permute-start = (bf16[128,256]{1,0:T(8,128)(2,1)S(1)}, bf16[128,256]{1,0:T(8,128)(2,1)S(1)}, u32[]{:S(2)}, u32[]{:S(2)}) collective-permute-start(bf16[128,256]{1,0:T(8,128)(2,1)S(1)} %get-tuple-element.10), channel_id=1, source_target_pairs={{0,2},{1,3},{2,0},{3,1},{4,6},{5,7},{6,4},{7,5},{8,10},{9,11},{10,... | collective-permute-start | bytes 196616 | tf_op jit(solution)/shard_map/ppermute | solution.py:490
  68.9 6.0 %copy-start = (bf16[128,256]{1,0:T(8,128)(2,1)S(1)}, bf16[128,256]{1,0:T(8,128)(2,1)}, u32[]{:S(2)}) copy-start(bf16[128,256]{1,0:T(8,128)(2,1)} %x_hbm.1) | copy-start | bytes 196612
